TPU v7x, 8 devices: a whole 2x2x1 slice. The times are simulated.
8 devices in a mesh: dp: 2 (over z, y), tp: 4 (over x, core).
Axes of the slice: x: 2, y: 2, z: 1, core: 2. Of those that a mesh axis runs over, the one named last changes fastest.
Arguments:
- x: bfloat16 [448, 5120], P('dp'), parts along dimension 0
- lengths: int32 [194], P('dp'), parts along dimension 0
- attn_gain: bfloat16 [2, 5120], replicated
- w_q: bfloat16 [2, 5120, 4096], P(None, None, 'tp')
- w_k: bfloat16 [2, 5120, 1024], P(None, None, 'tp')
- w_v: bfloat16 [2, 5120, 1024], P(None, None, 'tp')
- w_o: bfloat16 [2, 4096, 5120], P(None, 'tp')
- mlp_gain: bfloat16 [2, 5120], replicated
- w_gate: bfloat16 [2, 5120, 14336], P(None, None, 'tp')
- w_up: bfloat16 [2, 5120, 14336], P(None, None, 'tp')
- w_down: bfloat16 [2, 14336, 5120], P(None, 'tp')
- k_cache: bfloat16 [2, 194, 8, 256, 128], P(None, 'dp', 'tp'), parts along dimension 1
- v_cache: bfloat16 [2, 194, 8, 256, 128], P(None, 'dp', 'tp'), parts along dimension 1
Outputs:
- output: bfloat16 [448, 5120], P('dp'), parts along dimension 0
There are 2 independent parts. A program takes and returns all parts, laid end to end along the dimension named above; an argument that names none is the same for every part.
All inputs are finite; a program needn't handle non-finite values.
Results may differ from a plain program's by a relative error of at most 0.0199313.
Values are sent between devices in bfloat16 or wider.
A program may use at most 1.25 GiB of HBM per device.

v0:
```python
import jax
import jax.numpy as jnp
from jax import lax
from jax.sharding import PartitionSpec as P

ROPE_BASE = 500000.0
EPSILON = 1e-5


def rms_norm(x, norm_gain):
    x_f32 = x.astype(jnp.float32)
    inv_rms = lax.rsqrt(jnp.mean(x_f32 * x_f32, axis=-1, keepdims=True) + EPSILON)
    return (x_f32 * inv_rms * norm_gain.astype(jnp.float32)).astype(jnp.bfloat16)


def rope_tables(positions, head_dim):
    freq_exps = jnp.arange(0, head_dim, 2, dtype=jnp.float32) / head_dim
    angles = positions.astype(jnp.float32)[:, None] * jnp.power(ROPE_BASE, -freq_exps)[None, :]
    return jnp.cos(angles)[:, None, :], jnp.sin(angles)[:, None, :]


def apply_rope(vectors, cos_tab, sin_tab):
    half_dim = vectors.shape[-1] // 2
    vec_f32 = vectors.astype(jnp.float32)
    first = vec_f32[..., :half_dim]
    second = vec_f32[..., half_dim:]
    return jnp.concatenate([first * cos_tab - second * sin_tab, second * cos_tab + first * sin_tab], axis=-1).astype(jnp.bfloat16)


def project(normed, weight, head_dim):
    return jnp.dot(normed, weight, preferred_element_type=jnp.float32).astype(jnp.bfloat16).reshape(normed.shape[0], -1, head_dim)


def attention(q_rot, k_rot, v_new, k_cache, v_cache, lengths):
    dec_rows = lengths.shape[0] - 1
    kv_local = k_cache.shape[1]
    seq_len = k_cache.shape[2]
    head_dim = k_cache.shape[3]
    tok_count = q_rot.shape[0]
    chunk_len = tok_count - dec_rows
    attn_scale = head_dim ** -0.5
    q_grouped = q_rot.reshape(tok_count, kv_local, -1, head_dim)
    q_dec = q_grouped[:dec_rows]
    q_chk = q_grouped[dec_rows:]
    seq_ids = jnp.arange(seq_len)
    dec_cache = jnp.einsum('bgrd,bgsd->bgrs', q_dec, k_cache[:dec_rows], preferred_element_type=jnp.float32) * attn_scale
    dec_cache = jnp.where(seq_ids[None, None, None, :] < lengths[:dec_rows, None, None, None], dec_cache, -jnp.inf)
    dec_self = jnp.einsum('bgrd,bgd->bgr', q_dec, k_rot[:dec_rows], preferred_element_type=jnp.float32)[..., None] * attn_scale
    dec_prob = jax.nn.softmax(jnp.concatenate([dec_cache, dec_self], axis=-1), axis=-1).astype(jnp.bfloat16)
    dec_out = jnp.einsum('bgrs,bgsd->bgrd', dec_prob[..., :seq_len], v_cache[:dec_rows], preferred_element_type=jnp.float32) + dec_prob[..., seq_len:].astype(jnp.float32) * v_new[:dec_rows, :, None, :].astype(jnp.float32)
    chk_cache = jnp.einsum('cgrd,gsd->cgrs', q_chk, k_cache[dec_rows], preferred_element_type=jnp.float32) * attn_scale
    chk_cache = jnp.where(seq_ids[None, None, None, :] < lengths[dec_rows], chk_cache, -jnp.inf)
    chk_self = jnp.einsum('cgrd,jgd->cgrj', q_chk, k_rot[dec_rows:], preferred_element_type=jnp.float32) * attn_scale
    tok_ids = jnp.arange(chunk_len)
    causal_mask = tok_ids[None, :] <= tok_ids[:, None]
    chk_self = jnp.where(causal_mask[:, None, None, :], chk_self, -jnp.inf)
    chk_prob = jax.nn.softmax(jnp.concatenate([chk_cache, chk_self], axis=-1), axis=-1).astype(jnp.bfloat16)
    chk_out = jnp.einsum('cgrs,gsd->cgrd', chk_prob[..., :seq_len], v_cache[dec_rows], preferred_element_type=jnp.float32) + jnp.einsum('cgrj,jgd->cgrd', chk_prob[..., seq_len:], v_new[dec_rows:], preferred_element_type=jnp.float32)
    return jnp.concatenate([dec_out.reshape(dec_rows, -1), chk_out.reshape(chunk_len, -1)], axis=0).astype(jnp.bfloat16)


def decoder_layer(x, cos_tab, sin_tab, lengths, attn_gain, w_q, w_k, w_v, w_o, mlp_gain, w_gate, w_up, w_down, k_cache, v_cache):
    head_dim = k_cache.shape[-1]
    normed = rms_norm(x, attn_gain)
    q_rot = apply_rope(project(normed, w_q, head_dim), cos_tab, sin_tab)
    k_rot = apply_rope(project(normed, w_k, head_dim), cos_tab, sin_tab)
    v_new = project(normed, w_v, head_dim)
    attended = attention(q_rot, k_rot, v_new, k_cache, v_cache, lengths)
    attn_part = jnp.dot(attended, w_o, preferred_element_type=jnp.float32).astype(jnp.bfloat16)
    attn_sum = lax.psum(attn_part, 'tp')
    hidden = (x.astype(jnp.float32) + attn_sum.astype(jnp.float32)).astype(jnp.bfloat16)
    mlp_in = rms_norm(hidden, mlp_gain)
    gate_proj = jnp.dot(mlp_in, w_gate, preferred_element_type=jnp.float32)
    up_proj = jnp.dot(mlp_in, w_up, preferred_element_type=jnp.float32)
    activated = (jax.nn.silu(gate_proj) * up_proj).astype(jnp.bfloat16)
    mlp_part = jnp.dot(activated, w_down, preferred_element_type=jnp.float32).astype(jnp.bfloat16)
    mlp_sum = lax.psum(mlp_part, 'tp')
    return (hidden.astype(jnp.float32) + mlp_sum.astype(jnp.float32)).astype(jnp.bfloat16)


def solution(mesh):
    col_spec = P(None, None, 'tp')
    row_spec = P(None, 'tp', None)
    cache_spec = P(None, 'dp', 'tp', None, None)
    in_specs = (P('dp', None), P('dp'), P(), col_spec, col_spec, col_spec, row_spec, P(), col_spec, col_spec, row_spec, cache_spec, cache_spec)

    def body(x, lengths, attn_gain, w_q, w_k, w_v, w_o, mlp_gain, w_gate, w_up, w_down, k_cache, v_cache):
        dec_rows = lengths.shape[0] - 1
        chunk_len = x.shape[0] - dec_rows
        positions = jnp.concatenate([lengths[:dec_rows], lengths[dec_rows] + jnp.arange(chunk_len, dtype=jnp.int32)])
        cos_tab, sin_tab = rope_tables(positions, k_cache.shape[-1])
        hidden = x
        for layer_idx in range(w_q.shape[0]):
            hidden = decoder_layer(hidden, cos_tab, sin_tab, lengths, attn_gain[layer_idx], w_q[layer_idx], w_k[layer_idx], w_v[layer_idx], w_o[layer_idx], mlp_gain[layer_idx], w_gate[layer_idx], w_up[layer_idx], w_down[layer_idx], k_cache[layer_idx], v_cache[layer_idx])
        return hidden

    return jax.shard_map(body, mesh=mesh, in_specs=in_specs, out_specs=P('dp', None), check_vma=False)
```

profile of v0, /device:TPU:0, one launch (start us, length us, event | category | flops | bytes accessed | tf_op | source)
XLA Modules:
  0.0 443.1 jit_solution(7239687959496812294)
XLA Ops:
  9.1 2.2 fusion.66
  12.8 3.4 fusion.158
  16.9 5.7 %fusion.120 = f32[28,8,8,128]{3,1,2,0:T(8,128)S(1)} fusion(bf16[2,5120,1024]{2,1,0:T(8,128)(2,1)} %param.16, bf16[224,5120]{1,0:T(8,128)(2,1)S(1)} %copy-done.1, f32[5120]{0:T(1024)S(1)} %bitcast.289, f32[224]{0:T(256)S(1)} %add_rsqrt_fusion.3), kind=kOutput, calls=%fused_computation.114 | convolution fusion | flops 2353856512 | bytes 13718400 | tf_op jit(solution)/shard_map/dot_general | solution.py:31
  25.8 7.9 %fusion.24 = f32[96,2,4,256]{3,2,1,0:T(4,128)S(1)} fusion(bf16[96,2,4,128]{3,2,1,0:T(4,128)(2,1)S(1)} %bitcast.270, bf16[2,97,2,256,128]{4,3,2,1,0:T(8,128)(2,1)} %param.24), kind=kOutput, calls=%fused_computation.24 | convolution fusion | flops 50331648 | bytes 13565952 | tf_op jit(solution)/shard_map/bgrd,bgsd->bgrs/dot_general | solution.py:46
  37.9 6.3 %fusion.149 = bf16[96,2,4,128]{3,2,1,0:T(4,128)(2,1)S(1)} fusion(bf16[96,2,4,256]{3,2,1,0:T(4,128)(2,1)S(1)} %copy.97, bf16[2,97,2,256,128]{4,3,2,1,0:T(8,128)(2,1)} %param.25, f32[96,2,128]{2,1,0:T(2,128)S(1)} %reshape.244, f32[96,2,4]{2,1,0:T(2,128)S(1)} %copy.98), kind=kOutput, calls=%fused_computation.135 | convolution fusion | flops 50626560 | bytes 13274112 | tf_op jit(solution)/shard_map/bgrs,bgsd->bgrd/dot_general | solution.py:50
  48.7 8.0 %fusion.42 = bf16[224,5120]{1,0:T(8,128)(2,1)} fusion(bf16[2,1024,5120]{2,1,0:T(8,128)(2,1)} %param.19, bf16[128,1024]{0,1:T(8,128)(2,1)S(1)} %bitcast.273, bf16[96,1024]{0,1:T(8,128)(2,1)S(1)} %bitcast.275), kind=kOutput, calls=%fused_computation.54 | convolution fusion | flops 2350874624 | bytes 13238272 | tf_op jit(solution)/shard_map/dot_general | solution.py:69
  57.4 51.2 %all-reduce.5.cloned.1.call-done = bf16[224,5120]{1,0:T(8,128)(2,1)} async-done(((bf16[224,5120]{1,0:T(8,128)(2,1)}), bf16[224,5120]{1,0:T(8,128)(2,1)}) %all-reduce.5.cloned.1.call-update) | async-done | bytes 2293776 | tf_op jit(solution)/shard_map/psum | solution.py:70
  108.6 3.4 fusion.70
  112.0 15.5 %fusion.10 = f32[224,3584]{1,0:T(8,128)S(1)} fusion(bf16[2,5120,3584]{2,1,0:T(8,128)(2,1)} %param.21, bf16[224,5120]{1,0:T(8,128)(2,1)S(1)} %get-tuple-element.10, f32[5120]{0:T(1024)S(1)} %bitcast.291, f32[224]{0:T(256)S(1)} %add_rsqrt_fusion.2), kind=kOutput, calls=%fused_computation.10 | convolution fusion | flops 8225423360 | bytes 42226560 | tf_op jit(solution)/shard_map/dot_general | solution.py:73
  127.5 16.8 %fusion.63.clone.5 = bf16[224,3584]{1,0:T(8,128)(2,1)} fusion(bf16[2,5120,3584]{2,1,0:T(8,128)(2,1)} %param.22, f32[224,3584]{1,0:T(8,128)S(1)} %fusion.10, bf16[224,5120]{1,0:T(8,128)(2,1)S(1)} %get-tuple-element.10, f32[5120]{0:T(1024)S(1)} %bitcast.292, f32[224]{0:T(256)S(1)} %add_rsqrt_fusion.2), kind=kOutput, calls=%fused_computation.61.clone.clone.clone.2 | convolution fusion | flops 8230240256 | bytes 43832192 | tf_op jit(solution)/shard_map/dot_general | solution.py:74
  144.3 17.2 %fusion.48 = bf16[224,5120]{1,0:T(8,128)(2,1)} fusion(bf16[2,3584,5120]{2,1,0:T(8,128)(2,1)} %param.23, bf16[224,3584]{1,0:T(8,128)(2,1)} %fusion.63.clone.5), kind=kOutput, calls=%fused_computation.56 | convolution fusion | flops 8221982720 | bytes 40599552 | tf_op jit(solution)/shard_map/dot_general | solution.py:76
  161.7 48.9 %all-reduce.7.cloned.1.call-done = bf16[224,5120]{1,0:T(8,128)(2,1)} async-done(((bf16[224,5120]{1,0:T(8,128)(2,1)}), bf16[224,5120]{1,0:T(8,128)(2,1)}) %all-reduce.7.cloned.1.call-update) | async-done | bytes 2293776 | tf_op jit(solution)/shard_map/psum | solution.py:77
  210.6 2.6 fusion.74
  214.2 2.6 fusion.167
  218.9 6.6 %fusion.129 = f32[28,8,8,128]{3,1,2,0:T(8,128)S(1)} fusion(bf16[224,5120]{1,0:T(8,128)(2,1)S(1)} %fusion.76, bf16[2,5120,1024]{2,1,0:T(8,128)(2,1)} %param.16), kind=kOutput, calls=%fused_computation.117 | convolution fusion | flops 2349268992 | bytes 13697024 | tf_op jit(solution)/shard_map/dot_general | solution.py:31
  227.5 7.9 %fusion.20 = f32[96,2,4,256]{3,2,1,0:T(4,128)S(1)} fusion(bf16[96,2,4,128]{3,2,1,0:T(4,128)(2,1)S(1)} %bitcast.271, bf16[2,97,2,256,128]{4,3,2,1,0:T(8,128)(2,1)} %param.24), kind=kOutput, calls=%fused_computation.20 | convolution fusion | flops 50331648 | bytes 13565952 | tf_op jit(solution)/shard_map/bgrd,bgsd->bgrs/dot_general | solution.py:46
  236.2 1.9 fusion.200
  239.7 1.7 fusion.224
  242.2 1.7 broadcast_multiply_fusion
  250.2 1.7 fusion.232
  251.9 1.9 fusion.231
  255.5 2.1 copy.110
  258.5 7.1 %fusion.146 = bf16[96,2,4,128]{3,2,1,0:T(4,128)(2,1)} fusion(bf16[96,2,4,256]{3,2,1,0:T(4,128)(2,1)} %copy.110, bf16[2,97,2,256,128]{4,3,2,1,0:T(8,128)(2,1)} %param.25, f32[96,2,128]{2,1,0:T(2,128)} %reshape.250, f32[96,2,4]{2,1,0:T(2,128)S(1)} %copy.111), kind=kOutput, calls=%fused_computation.134 | convolution fusion | flops 50626560 | bytes 13274112 | tf_op jit(solution)/shard_map/bgrs,bgsd->bgrd/dot_general | solution.py:50
  265.5 1.8 copy.133
  271.7 8.0 %fusion.45 = bf16[224,5120]{1,0:T(8,128)(2,1)} fusion(bf16[2,1024,5120]{2,1,0:T(8,128)(2,1)} %param.19, bf16[128,1024]{0,1:T(8,128)(2,1)S(1)} %bitcast.274, bf16[96,1024]{0,1:T(8,128)(2,1)S(1)} %bitcast.276), kind=kOutput, calls=%fused_computation.55 | convolution fusion | flops 2350874624 | bytes 13238272 | tf_op jit(solution)/shard_map/dot_general | solution.py:69
  279.8 49.0 %all-reduce.9.cloned.1.call-done = bf16[224,5120]{1,0:T(8,128)(2,1)} async-done(((bf16[224,5120]{1,0:T(8,128)(2,1)}), bf16[224,5120]{1,0:T(8,128)(2,1)}) %all-reduce.9.cloned.1.call-update) | async-done | bytes 2293776 | tf_op jit(solution)/shard_map/psum | solution.py:70
  328.9 3.7 fusion.78
  332.6 17.1 %fusion.4 = f32[224,3584]{1,0:T(8,128)} fusion(bf16[2,5120,3584]{2,1,0:T(8,128)(2,1)} %param.21, bf16[224,5120]{1,0:T(8,128)(2,1)S(1)} %get-tuple-element.6, f32[5120]{0:T(1024)S(1)} %bitcast.286, f32[224]{0:T(256)S(1)} %add_rsqrt_fusion), kind=kOutput, calls=%fused_computation.4 | convolution fusion | flops 8225423360 | bytes 42226560 | tf_op jit(solution)/shard_map/dot_general | solution.py:73
  349.8 16.5 %fusion.60.clone.5 = bf16[224,3584]{1,0:T(8,128)(2,1)S(1)} fusion(bf16[2,5120,3584]{2,1,0:T(8,128)(2,1)} %param.22, f32[224,3584]{1,0:T(8,128)} %fusion.4, bf16[224,5120]{1,0:T(8,128)(2,1)S(1)} %get-tuple-element.6, f32[5120]{0:T(1024)S(1)} %bitcast.287, f32[224]{0:T(256)S(1)} %add_rsqrt_fusion), kind=kOutput, calls=%fused_computation.60.clone.clone.clone.2 | convolution fusion | flops 8230240256 | bytes 43832192 | tf_op jit(solution)/shard_map/dot_general | solution.py:74
  366.3 16.8 %fusion.51 = bf16[224,5120]{1,0:T(8,128)(2,1)} fusion(bf16[2,3584,5120]{2,1,0:T(8,128)(2,1)} %param.23, bf16[224,3584]{1,0:T(8,128)(2,1)S(1)} %fusion.60.clone.5), kind=kOutput, calls=%fused_computation.57 | convolution fusion | flops 8221982720 | bytes 40599552 | tf_op jit(solution)/shard_map/dot_general | solution.py:76
  383.1 49.1 %all-reduce.11.cloned.1.call-done = bf16[224,5120]{1,0:T(8,128)(2,1)} async-done(((bf16[224,5120]{1,0:T(8,128)(2,1)}), bf16[224,5120]{1,0:T(8,128)(2,1)}) %all-reduce.11.cloned.1.call-update) | async-done | bytes 2293776 | tf_op jit(solution)/shard_map/psum | solution.py:77
  432.2 3.9 fusion.81
  (139 shorter events, 38.8 us)
Async XLA Ops:
  6.5 102.0 %all-reduce.5.cloned.1.call-start = ((), (), s32[]{:S(2)}) async-start(), calls=%async_computation | async-start | bytes 4587520 | tf_op jit(solution)/shard_map/psum | solution.py:70
  8.4 36.5 %copy-start.18 = (pred[256]{0:T(512)(128)(4,1)}, pred[256]{0:T(512)(128)(4,1)S(1)}, u32[]{:S(2)}) copy-start(pred[256]{0:T(512)(128)(4,1)S(1)} %iota_compare_fusion.2) | copy-start | bytes 772
  9.1 35.3 %copy-start.11 = (pred[128,128]{1,0:T(8,128)(4,1)}, pred[128,128]{1,0:T(8,128)(4,1)S(1)}, u32[]{:S(2)}) copy-start(pred[128,128]{1,0:T(8,128)(4,1)S(1)} %iota_compare_fusion.1) | copy-start | bytes 49156
  12.8 3.4 copy-start.20
  12.8 4.1 copy-start.1
  16.2 0.6 copy-start.10
  16.8 7.2 %slice-start.1 = ((s8[5242880]{0:T(1024)(128)(4,1)}), s8[4194304]{0:T(1024)(128)(4,1)S(1)}, s32[]{:S(2)}) async-start(s8[5242880]{0:T(1024)(128)(4,1)} %bitcast.295), calls=%async_computation.5 | async-start | bytes 8388608
  16.9 7.1 %slice-start.2 = ((s8[5242880]{0:T(1024)(128)(4,1)}), s8[1048576]{0:T(1024)(128)(4,1)S(1)}, s32[]{:S(2)}) async-start(s8[5242880]{0:T(1024)(128)(4,1)} %bitcast.295), calls=%async_computation.6 | async-start | bytes 2097152
  34.3 2.3 slice-start
  48.7 8.1 %copy-start.14 = (bf16[2,5120]{1,0:T(2,128)(2,1)S(1)}, bf16[2,5120]{1,0:T(2,128)(2,1)}, u32[]{:S(2)}) copy-start(bf16[2,5120]{1,0:T(2,128)(2,1)} %param.20) | copy-start | bytes 61444
  56.7 153.9 %all-reduce.7.cloned.1.call-start = ((), (), s32[]{:S(2)}) async-start(), calls=%async_computation.1 | async-start | bytes 4587520 | tf_op jit(solution)/shard_map/psum | solution.py:77
  161.5 51.8 %copy-start.13 = (f32[1,5120]{1,0:T(1,128)S(1)}, f32[1,5120]{1,0:T(1,128)}, u32[]{:S(2)}) copy-start(f32[1,5120]{1,0:T(1,128)} %get-tuple-element.32) | copy-start | bytes 61444
  161.5 167.4 %all-reduce.9.cloned.1.call-start = ((), (), s32[]{:S(2)}) async-start(), calls=%async_computation.2 | async-start | bytes 4587520 | tf_op jit(solution)/shard_map/psum | solution.py:70
  210.6 2.6 copy-start
  210.6 7.5 %slice-start.3 = ((s8[5242880]{0:T(1024)(128)(4,1)}), s8[4194304]{0:T(1024)(128)(4,1)S(1)}, s32[]{:S(2)}) async-start(s8[5242880]{0:T(1024)(128)(4,1)} %bitcast.297), calls=%async_computation.7 | async-start | bytes 8388608
  213.3 4.8 %slice-start.4 = ((s8[5242880]{0:T(1024)(128)(4,1)}), s8[1048576]{0:T(1024)(128)(4,1)S(1)}, s32[]{:S(2)}) async-start(s8[5242880]{0:T(1024)(128)(4,1)} %bitcast.297), calls=%async_computation.8 | async-start | bytes 2097152
  226.2 9.2 %copy-start.7 = (bf16[96,8,128]{2,1,0:T(8,128)(2,1)}, bf16[96,8,128]{2,1,0:T(8,128)(2,1)S(1)}, u32[]{:S(2)}) copy-start(bf16[96,8,128]{2,1,0:T(8,128)(2,1)S(1)} %pad_maximum_fusion.2) | copy-start | bytes 589828
  235.5 0.6 copy-start.5
  246.1 4.1 copy-start.4
  246.1 4.1 copy-start.6
  246.1 4.1 copy-start.12
  246.1 5.9 %copy-start.19 = (pred[256]{0:T(512)(128)(4,1)S(1)}, pred[256]{0:T(512)(128)(4,1)}, u32[]{:S(2)}) copy-start(pred[256]{0:T(512)(128)(4,1)} %copy-done.18) | copy-start | bytes 772
  246.1 7.8 %copy-start.8 = (f32[96,256]{1,0:T(8,128)S(1)}, f32[96,256]{1,0:T(8,128)}, u32[]{:S(2)}) copy-start(f32[96,256]{1,0:T(8,128)} %slice_convert_fusion) | copy-start | bytes 294916
  258.4 8.9 %copy-start.16 = (f32[128,2,4]{0,2,1:T(4,128)S(1)}, f32[128,2,4]{0,2,1:T(4,128)}, u32[]{:S(2)}) copy-start(f32[128,2,4]{0,2,1:T(4,128)} %get-tuple-element.41) | copy-start | bytes 12292
  258.4 8.9 %copy-start.17 = (f32[128,2,4]{0,2,1:T(4,128)S(1)}, f32[128,2,4]{0,2,1:T(4,128)}, u32[]{:S(2)}) copy-start(f32[128,2,4]{0,2,1:T(4,128)} %get-tuple-element.39) | copy-start | bytes 12292
  267.3 4.4 copy-start.9
  279.8 52.8 %copy-start.15 = (f32[1,5120]{1,0:T(1,128)S(1)}, f32[1,5120]{1,0:T(1,128)}, u32[]{:S(2)}) copy-start(f32[1,5120]{1,0:T(1,128)} %get-tuple-element.29) | copy-start | bytes 61444
  279.8 152.4 %all-reduce.11.cloned.1.call-start = ((), (), s32[]{:S(2)}) async-start(), calls=%async_computation.3 | async-start | bytes 4587520 | tf_op jit(solution)/shard_map/psum | solution.py:77
  332.6 17.2 %copy-start.2 = (bf16[224,5120]{1,0:T(8,128)(2,1)}, bf16[224,5120]{1,0:T(8,128)(2,1)S(1)}, u32[]{:S(2)}) copy-start(bf16[224,5120]{1,0:T(8,128)(2,1)S(1)} %get-tuple-element.6) | copy-start | bytes 6881284
  383.0 49.1 %copy-start.3 = (bf16[224,5120]{1,0:T(8,128)(2,1)S(1)}, bf16[224,5120]{1,0:T(8,128)(2,1)}, u32[]{:S(2)}) copy-start(bf16[224,5120]{1,0:T(8,128)(2,1)} %copy-done.2) | copy-start | bytes 6881284
Sparse Core Ops, SparseCore 0:
  56.9 51.6 all-reduce.4
  161.6 48.9 all-reduce.6
  279.9 48.9 all-reduce.8
  383.2 48.9 all-reduce.10
where the time goes:
time: 451 us; the launch traced here: 443 us
  waiting for transfers between devices  198 us (44%)
  matrix products  175 us (39%)
  other arithmetic  35.9 us (8%)
  local copies, waits for them, and re-layouts  18.9 us (4%)
  between operations  14.2 us (3%)
    psum x2, waiting for transfers between devices, decoder_layer(): attn_sum = lax.psum(attn_part, 'tp')  100 us
    psum x2, waiting for transfers between devices, decoder_layer(): mlp_sum = lax.psum(mlp_part, 'tp')  98 us
    dot_general x2, matrix products, decoder_layer(): jnp.dot(activated, w_down, preferred_element_type=jnp.float32)  34 us
    dot_general x2, matrix products, decoder_layer(): up_proj = jnp.dot(mlp_in, w_up, preferred_element_type=jnp.float32)  33.3 us
    dot_general x2, matrix products, decoder_layer(): gate_proj = jnp.dot(mlp_in, w_gate, preferred_element_type=jnp.float32)  32.6 us
    dot_general x6, matrix products, project(): jnp.dot(normed, weight, preferred_element_type=jnp.float32)  19.7 us
    dot_general x2, matrix products, decoder_layer(): jnp.dot(attended, w_o, preferred_element_type=jnp.float32)  16.1 us
    dot_general x2, matrix products, attention(): jnp.einsum('bgrd,bgsd->bgrs', q_dec, k_cache[:dec_rows], preferred_elemen...  15.8 us
  transfers between devices with their start and end apart: 4, of which 4 were waited for; matrix products, arithmetic and copies ran while one was open for 0% of the time, Pallas kernels for 0%

commit v1 on v0

--- a/solution.py
+++ b/solution.py
@@ -1,10 +1,20 @@
+import functools
+
 import jax
 import jax.numpy as jnp
 from jax import lax
+from jax.experimental import pallas as pl
+from jax.experimental.pallas import tpu as pltpu
 from jax.sharding import PartitionSpec as P
 
 ROPE_BASE = 500000.0
 EPSILON = 1e-5
+MESH = pl.DeviceIdType.MESH
+F32 = jnp.float32
+BF16 = jnp.bfloat16
+CW = 512
+G_SLOTS = 3
+D_SLOTS = 4
 
 
 def rms_norm(x, norm_gain):
@@ -25,10 +35,6 @@
     first = vec_f32[..., :half_dim]
     second = vec_f32[..., half_dim:]
     return jnp.concatenate([first * cos_tab - second * sin_tab, second * cos_tab + first * sin_tab], axis=-1).astype(jnp.bfloat16)
-
-
-def project(normed, weight, head_dim):
-    return jnp.dot(normed, weight, preferred_element_type=jnp.float32).astype(jnp.bfloat16).reshape(normed.shape[0], -1, head_dim)
 
 
 def attention(q_rot, k_rot, v_new, k_cache, v_cache, lengths):
@@ -59,23 +65,290 @@
     return jnp.concatenate([dec_out.reshape(dec_rows, -1), chk_out.reshape(chunk_len, -1)], axis=0).astype(jnp.bfloat16)
 
 
-def decoder_layer(x, cos_tab, sin_tab, lengths, attn_gain, w_q, w_k, w_v, w_o, mlp_gain, w_gate, w_up, w_down, k_cache, v_cache):
-    head_dim = k_cache.shape[-1]
-    normed = rms_norm(x, attn_gain)
-    q_rot = apply_rope(project(normed, w_q, head_dim), cos_tab, sin_tab)
-    k_rot = apply_rope(project(normed, w_k, head_dim), cos_tab, sin_tab)
-    v_new = project(normed, w_v, head_dim)
-    attended = attention(q_rot, k_rot, v_new, k_cache, v_cache, lengths)
-    attn_part = jnp.dot(attended, w_o, preferred_element_type=jnp.float32).astype(jnp.bfloat16)
-    attn_sum = lax.psum(attn_part, 'tp')
-    hidden = (x.astype(jnp.float32) + attn_sum.astype(jnp.float32)).astype(jnp.bfloat16)
-    mlp_in = rms_norm(hidden, mlp_gain)
-    gate_proj = jnp.dot(mlp_in, w_gate, preferred_element_type=jnp.float32)
-    up_proj = jnp.dot(mlp_in, w_up, preferred_element_type=jnp.float32)
-    activated = (jax.nn.silu(gate_proj) * up_proj).astype(jnp.bfloat16)
-    mlp_part = jnp.dot(activated, w_down, preferred_element_type=jnp.float32).astype(jnp.bfloat16)
-    mlp_sum = lax.psum(mlp_part, 'tp')
-    return (hidden.astype(jnp.float32) + mlp_sum.astype(jnp.float32)).astype(jnp.bfloat16)
+def layer_kernel(layer, fuse_next, att, x, gain_mlp, gain_next, wo, wg, wu, wd, wq, wk, wv, *rest):
+    if fuse_next:
+        y, qkv = rest[:2]
+        rest = rest[2:]
+    else:
+        y = rest[0]
+        rest = rest[1:]
+    gbuf, dbuf, acc, act, pbuf, rbuf, sbuf, xb1, xb2, h1, h2, ssq, pre, wo_sem, g_sem, d_sem, y_sem, p_ss, p_rs, x_ss, x_rs, h_ss, h_rs = rest
+    rows, width = x.shape
+    half = rows // 2
+    ff = wg.shape[2]
+    n_chunks = width // CW
+    o_depth = wo.shape[1]
+    o_per_slot = ff // o_depth
+    dp_me = lax.axis_index('dp')
+    me = lax.axis_index('tp')
+    core = lax.rem(me, 2)
+    core_peer = (dp_me, me + 1 - 2 * core)
+    x_peer = (dp_me, lax.rem(me + 2, 4))
+    own = pl.ds(pl.multiple_of(core * half, 16), half)
+    oth = pl.ds(pl.multiple_of((1 - core) * half, 16), half)
+    xbs = (xb1, xb2)
+    hs = (h1, h2)
+
+    def cols(j):
+        return pl.ds(pl.multiple_of(j * CW, CW), CW)
+
+    def wo_copy(j):
+        return pltpu.make_async_copy(wo.at[layer, :, cols(j)], dbuf.at[j // o_per_slot, pl.ds(pl.multiple_of(lax.rem(j, o_per_slot) * o_depth, 16), o_depth), :], wo_sem.at[j])
+
+    def g_copies(j):
+        slot = lax.rem(j, G_SLOTS)
+        return (pltpu.make_async_copy(wg.at[layer, cols(j), :], gbuf.at[slot, 0], g_sem.at[slot, 0]),
+                pltpu.make_async_copy(wu.at[layer, cols(j), :], gbuf.at[slot, 1], g_sem.at[slot, 1]))
+
+    def d_copy(j):
+        slot = lax.rem(j, D_SLOTS)
+        return pltpu.make_async_copy(wd.at[layer, :, cols(j)], dbuf.at[slot], d_sem.at[slot])
+
+    def p_copy(ar, j):
+        return pltpu.make_async_remote_copy(pbuf.at[j, oth, :], rbuf.at[j], p_ss.at[ar, j], p_rs.at[ar, j], device_id=core_peer, device_id_type=MESH)
+
+    def x_copy(ar, j):
+        return pltpu.make_async_remote_copy(sbuf.at[j], xbs[ar].at[j], x_ss.at[ar, j], x_rs.at[ar, j], device_id=x_peer, device_id_type=MESH)
+
+    def h_copy(ar, j):
+        return pltpu.make_async_remote_copy(hs[ar].at[j, own, :], hs[ar].at[j, own, :], h_ss.at[ar, j], h_rs.at[ar, j], device_id=core_peer, device_id_type=MESH)
+
+    def h_wait(ar, j):
+        pltpu.make_async_remote_copy(hs[ar].at[j, oth, :], hs[ar].at[j, oth, :], h_ss.at[ar, j], h_rs.at[ar, j], device_id=core_peer, device_id_type=MESH).wait_recv()
+
+    def send_part(ar, j, part):
+        pbuf[j] = part.astype(BF16)
+        p_copy(ar, j).start()
+
+    def pair_sum(ar, j):
+        p_copy(ar, j).wait_recv()
+        sbuf[j] = (pbuf[j, own, :].astype(F32) + rbuf[j].astype(F32)).astype(BF16)
+        x_copy(ar, j).start()
+
+    def finish(ar, j):
+        x_copy(ar, j).wait_recv()
+        total = sbuf[j].astype(F32) + xbs[ar][j].astype(F32)
+        resid = x[own, cols(j)] if ar == 0 else h1[j, own, :]
+        hs[ar][j, own, :] = (resid.astype(F32) + total).astype(BF16)
+        h_copy(ar, j).start()
+
+    def add_squares(vals):
+        sq = vals * vals
+        ssq[...] += sq[:, :128] + sq[:, 128:256] + sq[:, 256:384] + sq[:, 384:]
+
+    def inv_rms():
+        return lax.rsqrt(jnp.sum(ssq[...], axis=-1, keepdims=True) * (1.0 / width) + EPSILON)
+
+    for j in range(n_chunks):
+        wo_copy(j).start()
+    for j in range(G_SLOTS):
+        for c in g_copies(j):
+            c.start()
+    barrier = pltpu.get_barrier_semaphore()
+    for peer in (core_peer, x_peer):
+        pl.semaphore_signal(barrier, inc=1, device_id=peer, device_id_type=MESH)
+
+    ssq[...] = jnp.zeros_like(ssq)
+
+    def sq_step(j, c):
+        add_squares(x[:, cols(j)].astype(F32))
+        return c
+
+    lax.fori_loop(0, n_chunks, sq_step, 0)
+    pre[...] = jnp.broadcast_to(jnp.maximum(inv_rms(), 1e-30), pre.shape)
+    ssq[...] = jnp.zeros_like(ssq)
+    acc[...] = jnp.zeros_like(acc)
+    pl.semaphore_wait(barrier, 2)
+
+    def o_step(j, c):
+        wo_copy(j).wait()
+        w = dbuf[j // o_per_slot, pl.ds(pl.multiple_of(lax.rem(j, o_per_slot) * o_depth, 16), o_depth), :]
+        send_part(0, j, jnp.dot(att[...], w, preferred_element_type=F32))
+
+        @pl.when(j >= 1)
+        def _():
+            pair_sum(0, j - 1)
+        return c
+
+    lax.fori_loop(0, n_chunks, o_step, 0)
+    pair_sum(0, n_chunks - 1)
+
+    def gu_block(j):
+        h_wait(0, j)
+        vals = h1[j].astype(F32)
+        add_squares(vals)
+        a = (vals * pre[:, :1] * gain_mlp[:, cols(j)]).astype(BF16)
+        slot = lax.rem(j, G_SLOTS)
+        for c in g_copies(j):
+            c.wait()
+
+        def mat(m, c):
+            for n in range(ff // CW):
+                col = pl.ds(pl.multiple_of(m * ff + n * CW, CW), CW)
+                acc[:, col] += jnp.dot(a, gbuf[slot, m, :, n * CW:(n + 1) * CW], preferred_element_type=F32)
+            return c
+
+        lax.fori_loop(0, 2, mat, 0)
+
+        @pl.when(j + G_SLOTS < n_chunks)
+        def _():
+            for c in g_copies(j + G_SLOTS):
+                c.start()
+
+        @pl.when(j >= n_chunks - D_SLOTS)
+        def _():
+            d_copy(j - (n_chunks - D_SLOTS)).start()
+
+    def gu_step(j, c):
+        finish(0, j)
+
+        @pl.when(j >= 1)
+        def _():
+            gu_block(j - 1)
+        return c
+
+    lax.fori_loop(0, n_chunks, gu_step, 0)
+    gu_block(n_chunks - 1)
+
+    q_cols, k_cols = wq.shape[2], wk.shape[2]
+    n_qkv = q_cols + 2 * k_cols
+
+    def qkv_copies(j):
+        slot, which, side = j // 4, lax.rem(j // 2, 2), lax.rem(j, 2)
+        base = side * (ff // 2)
+        dst = gbuf.at[slot, which]
+        sem = wo_sem.at[j]
+        return (pltpu.make_async_copy(wq.at[layer + 1, cols(j), :], dst.at[:, pl.ds(pl.multiple_of(base, 128), q_cols)], sem),
+                pltpu.make_async_copy(wk.at[layer + 1, cols(j), :], dst.at[:, pl.ds(pl.multiple_of(base + q_cols, 128), k_cols)], qk_sem.at[0, j]),
+                pltpu.make_async_copy(wv.at[layer + 1, cols(j), :], dst.at[:, pl.ds(pl.multiple_of(base + q_cols + k_cols, 128), k_cols)], qk_sem.at[1, j]))
+
+    qk_sem = y_sem
+
+    scale = inv_rms() / pre[:, :1]
+    pre[...] = jnp.broadcast_to(jnp.maximum(inv_rms(), 1e-30), pre.shape)
+
+    def act_step(n, c):
+        gate = acc[:, cols(n)] * scale
+        up = acc[:, pl.ds(pl.multiple_of(ff + n * CW, CW), CW)] * scale
+        act[:, cols(n)] = (gate * jax.nn.sigmoid(gate) * up).astype(BF16)
+        return c
+
+    lax.fori_loop(0, ff // CW, act_step, 0)
+
+    for j in range(n_chunks):
+        p_copy(0, j).wait_send()
+        x_copy(0, j).wait_send()
+
+    def d_step(j, c):
+        d_copy(j).wait()
+        send_part(1, j, jnp.dot(act[...], dbuf[lax.rem(j, D_SLOTS)], preferred_element_type=F32))
+
+        @pl.when(j + D_SLOTS < n_chunks)
+        def _():
+            d_copy(j + D_SLOTS).start()
+
+        if fuse_next:
+            for c2 in qkv_copies(j):
+                c2.start()
+
+        @pl.when(j >= 1)
+        def _():
+            pair_sum(1, j - 1)
+        return c
+
+    lax.fori_loop(0, n_chunks, d_step, 0)
+    pair_sum(1, n_chunks - 1)
+
+    def out_copy(j):
+        return pltpu.make_async_copy(h2.at[j], y.at[:, cols(j)], h_ss.at[2, j])
+
+    if fuse_next:
+        ssq[...] = jnp.zeros_like(ssq)
+        acc[:, :n_qkv] = jnp.zeros((rows, n_qkv), F32)
+
+    def last_block(j):
+        h_wait(1, j)
+        out_copy(j).start()
+        if fuse_next:
+            vals = h2[j].astype(F32)
+            add_squares(vals)
+            a = (vals * pre[:, :1] * gain_next[:, cols(j)]).astype(BF16)
+            for c in qkv_copies(j):
+                c.wait()
+            slot, which, side = j // 4, lax.rem(j // 2, 2), lax.rem(j, 2)
+            base = side * (ff // 2)
+            for n in range(n_qkv // CW):
+                col = pl.ds(pl.multiple_of(base + n * CW, 128), CW)
+                acc[:, n * CW:(n + 1) * CW] += jnp.dot(a, gbuf[slot, which, :, col], preferred_element_type=F32)
+
+    def last_step(j, c):
+        finish(1, j)
+
+        @pl.when(j >= 1)
+        def _():
+            last_block(j - 1)
+        return c
+
+    lax.fori_loop(0, n_chunks, last_step, 0)
+    last_block(n_chunks - 1)
+    if fuse_next:
+        scale2 = inv_rms() / pre[:, :1]
+        qkv[...] = (acc[:, :n_qkv] * scale2).astype(BF16)
+    for j in range(n_chunks):
+        out_copy(j).wait()
+        h_copy(0, j).wait_send()
+        h_copy(1, j).wait_send()
+        p_copy(1, j).wait_send()
+        x_copy(1, j).wait_send()
+
+
+def layer_call(layer, fuse_next, att, x, gain_mlp, gain_next, wo, wg, wu, wd, wq, wk, wv):
+    rows, width = x.shape
+    ff = wg.shape[2]
+    n_chunks = width // CW
+    half = rows // 2
+    n_qkv = wq.shape[2] + 2 * wk.shape[2]
+    vmem = pl.BlockSpec(memory_space=pltpu.VMEM)
+    hbm = pl.BlockSpec(memory_space=pl.ANY)
+    out_shape = [jax.ShapeDtypeStruct((rows, width), BF16)]
+    out_specs = [hbm]
+    if fuse_next:
+        out_shape.append(jax.ShapeDtypeStruct((rows, n_qkv), BF16))
+        out_specs.append(vmem)
+    sem = pltpu.SemaphoreType.DMA
+    return pl.pallas_call(
+        functools.partial(layer_kernel, layer, fuse_next),
+        out_shape=out_shape,
+        in_specs=[vmem] * 4 + [hbm] * 7,
+        out_specs=out_specs,
+        scratch_shapes=[
+            pltpu.VMEM((G_SLOTS, 2, CW, ff), BF16),
+            pltpu.VMEM((D_SLOTS, ff, CW), BF16),
+            pltpu.VMEM((rows, 2 * ff), F32),
+            pltpu.VMEM((rows, ff), BF16),
+            pltpu.VMEM((n_chunks, rows, CW), BF16),
+            pltpu.VMEM((n_chunks, half, CW), BF16),
+            pltpu.VMEM((n_chunks, half, CW), BF16),
+            pltpu.VMEM((n_chunks, half, CW), BF16),
+            pltpu.VMEM((n_chunks, half, CW), BF16),
+            pltpu.VMEM((n_chunks, rows, CW), BF16),
+            pltpu.VMEM((n_chunks, rows, CW), BF16),
+            pltpu.VMEM((rows, 128), F32),
+            pltpu.VMEM((rows, 128), F32),
+            sem((n_chunks,)),
+            sem((G_SLOTS, 2)),
+            sem((D_SLOTS,)),
+            sem((2, n_chunks)),
+            sem((2, n_chunks)),
+            sem((2, n_chunks)),
+            sem((2, n_chunks)),
+            sem((2, n_chunks)),
+            sem((3, n_chunks)),
+            sem((2, n_chunks)),
+        ],
+        compiler_params=pltpu.CompilerParams(collective_id=layer, has_side_effects=True, vmem_limit_bytes=67043328),
+        name='layer' + str(layer),
+    )(att, x, gain_mlp, gain_next, wo, wg, wu, wd, wq, wk, wv)
 
 
 def solution(mesh):
@@ -86,12 +359,26 @@
 
     def body(x, lengths, attn_gain, w_q, w_k, w_v, w_o, mlp_gain, w_gate, w_up, w_down, k_cache, v_cache):
         dec_rows = lengths.shape[0] - 1
-        chunk_len = x.shape[0] - dec_rows
+        rows = x.shape[0]
+        chunk_len = rows - dec_rows
+        head_dim = k_cache.shape[-1]
         positions = jnp.concatenate([lengths[:dec_rows], lengths[dec_rows] + jnp.arange(chunk_len, dtype=jnp.int32)])
-        cos_tab, sin_tab = rope_tables(positions, k_cache.shape[-1])
+        cos_tab, sin_tab = rope_tables(positions, head_dim)
+        n_layers = w_q.shape[0]
         hidden = x
-        for layer_idx in range(w_q.shape[0]):
-            hidden = decoder_layer(hidden, cos_tab, sin_tab, lengths, attn_gain[layer_idx], w_q[layer_idx], w_k[layer_idx], w_v[layer_idx], w_o[layer_idx], mlp_gain[layer_idx], w_gate[layer_idx], w_up[layer_idx], w_down[layer_idx], k_cache[layer_idx], v_cache[layer_idx])
+        normed = rms_norm(x, attn_gain[0])
+        q, k, v = (jnp.dot(normed, w[0], preferred_element_type=F32).astype(BF16) for w in (w_q, w_k, w_v))
+        for layer in range(n_layers):
+            q_rot = apply_rope(q.reshape(rows, -1, head_dim), cos_tab, sin_tab)
+            k_rot = apply_rope(k.reshape(rows, -1, head_dim), cos_tab, sin_tab)
+            att = attention(q_rot, k_rot, v.reshape(rows, -1, head_dim), k_cache[layer], v_cache[layer], lengths)
+            fuse_next = layer + 1 < n_layers
+            gain_next = attn_gain[min(layer + 1, n_layers - 1)][None].astype(F32)
+            outs = layer_call(layer, fuse_next, att, hidden, mlp_gain[layer][None].astype(F32), gain_next, w_o, w_gate, w_up, w_down, w_q, w_k, w_v)
+            hidden = outs[0]
+            if fuse_next:
+                nq, nk = w_q.shape[2], w_k.shape[2]
+                q, k, v = outs[1][:, :nq], outs[1][:, nq:nq + nk], outs[1][:, nq + nk:]
         return hidden
 
     return jax.shard_map(body, mesh=mesh, in_specs=in_specs, out_specs=P('dp', None), check_vma=False)

time: 451 us -> 217 us (0.48); the launches traced: 443 us -> 216 us
  waiting for transfers between devices: 198 us -> 0 us
  Pallas kernels: 0 us -> 141 us
  matrix products: 175 us -> 46.5 us
  other arithmetic: 35.9 us -> 16.9 us
  between operations: 14.2 us -> 0.65 us
  local copies, waits for them, and re-layouts: 18.9 us -> 11.3 us
    psum x4 -> x0, waiting for transfers between devices: 198 us -> none  [the longest x2 100 us: decoder_layer(): attn_sum = lax.psum(attn_part, 'tp')]
    pallas_call x0 -> x2, Pallas kernels: none -> 141 us  [layer_call(): pl.pallas_call(functools.partial(layer_kernel, layer, fuse_next), out_sha...]
    dot_general x14 -> x3, matrix products: 136 us -> 10.8 us  [body(): jnp.dot(normed, w[0], preferred_element_type=F32).astype(BF16)]
    reduce_sum x4 -> x1, other arithmetic: 11.9 us -> 2.19 us  [rms_norm(): jnp.mean(x_f32 * x_f32, axis=-1, keepdims=True) + EPSILON]
  transfers between devices with their start and end apart: 4 -> 0, of which waited for: 4 -> 0; matrix products, arithmetic and copies ran while one was open for 0% -> 0% of each run, Pallas kernels for 0% -> 0%
where the time goes in v1:
time: 217 us; the launch traced here: 216 us
  Pallas kernels  141 us (65%)
  matrix products  46.5 us (21%)
  other arithmetic  16.9 us (8%)
  local copies, waits for them, and re-layouts  11.3 us (5%)
    pallas_call x2, Pallas kernels, layer_call(): pl.pallas_call(functools.partial(layer_kernel, layer, fuse_next), out_sha...  141 us
    dot_general x2, matrix products, attention(): jnp.einsum('bgrd,bgsd->bgrs', q_dec, k_cache[:dec_rows], preferred_elemen...  15.8 us
    dot_general x2, matrix products, attention(): jnp.einsum('bgrs,bgsd->bgrd', dec_prob[..., :seq_len], v_cache[:dec_rows]...  12.6 us
    dot_general x3, matrix products, body(): jnp.dot(normed, w[0], preferred_element_type=F32).astype(BF16)  10.8 us

profile of v1, /device:TPU:0, one launch (start us, length us, event | category | flops | bytes accessed | tf_op | source)
XLA Modules:
  0.0 216.1 jit_solution(1207108196218073464)
XLA Ops:
  0.0 1.4 slice.201
  1.4 0.6 iota_compare_fusion.2
  2.1 0.7 iota_add_fusion
  2.7 0.7 add_convert_fusion.4
  3.5 2.2 %fusion.15 = f32[224]{0:T(256)S(1)} fusion(bf16[224,5120]{1,0:T(8,128)(2,1)} %x.1), kind=kLoop, calls=%fused_computation.17 | loop fusion | flops 3440416 | bytes 2294656 | tf_op jit(solution)/shard_map/reduce_sum | solution.py:22
  5.8 0.7 slice_convert_fusion.3
  6.4 2.5 %fusion.65 = bf16[224,256]{1,0:T(8,128)(2,1)S(1)} fusion(bf16[2,5120,256]{2,1,0:T(8,128)(2,1)} %wv.3, bf16[224,5120]{1,0:T(8,128)(2,1)S(1)} %copy-done, f32[5120]{0:T(1024)S(1)} %bitcast.194, f32[224]{0:T(256)S(1)} %add_rsqrt_fusion), kind=kOutput, calls=%fused_computation.61 | convolution fusion | flops 591847424 | bytes 5051264 | tf_op jit(solution)/shard_map/dot_general | solution.py:370
  9.7 2.6 %fusion.62 = f32[224,256]{1,0:T(8,128)S(1)} fusion(bf16[2,5120,256]{2,1,0:T(8,128)(2,1)} %wk.3, bf16[224,5120]{1,0:T(8,128)(2,1)S(1)} %copy-done, f32[5120]{0:T(1024)S(1)} %bitcast.195, f32[224]{0:T(256)S(1)} %add_rsqrt_fusion), kind=kOutput, calls=%fused_computation.60 | convolution fusion | flops 591904768 | bytes 5165952 | tf_op jit(solution)/shard_map/dot_general | solution.py:370
  13.0 5.7 %fusion.36 = f32[28,8,8,128]{3,1,2,0:T(8,128)S(1)} fusion(bf16[2,5120,1024]{2,1,0:T(8,128)(2,1)} %wq.3, bf16[224,5120]{1,0:T(8,128)(2,1)S(1)} %copy-done, f32[5120]{0:T(1024)S(1)} %bitcast.196, f32[224]{0:T(256)S(1)} %add_rsqrt_fusion), kind=kOutput, calls=%fused_computation.40 | convolution fusion | flops 2353856512 | bytes 13718400 | tf_op jit(solution)/shard_map/dot_general | solution.py:370
  20.5 7.9 %fusion.6 = f32[96,2,4,256]{3,2,1,0:T(4,128)S(1)} fusion(bf16[96,2,4,128]{3,2,1,0:T(4,128)(2,1)S(1)} %bitcast.185, bf16[2,97,2,256,128]{4,3,2,1,0:T(8,128)(2,1)} %param.24), kind=kOutput, calls=%fused_computation.6 | convolution fusion | flops 50331648 | bytes 13565952 | tf_op jit(solution)/shard_map/bgrd,bgsd->bgrs/dot_general | solution.py:52
  28.4 0.6 copy.93
  29.9 0.6 fusion.75
  31.8 6.3 %fusion.56 = bf16[96,2,4,128]{3,2,1,0:T(4,128)(2,1)S(1)} fusion(bf16[96,2,4,256]{3,2,1,0:T(4,128)(2,1)S(1)} %copy.99, bf16[2,97,2,256,128]{4,3,2,1,0:T(8,128)(2,1)} %param.25, f32[96,2,128]{2,1,0:T(2,128)S(1)} %reshape.220, f32[96,2,4]{2,1,0:T(2,128)S(1)} %copy.100), kind=kOutput, calls=%fused_computation.58 | convolution fusion | flops 50626560 | bytes 13274112 | tf_op jit(solution)/shard_map/bgrs,bgsd->bgrd/dot_general | solution.py:56
  38.3 1.3 fusion.109
  39.6 0.5 fusion.69
  40.5 1.2 convolution_bitcast_fusion.3
  42.1 0.8 pad_maximum_fusion.att
  42.9 71.9 %layer0.1 = (bf16[224,5120]{1,0:T(8,128)(2,1)}, bf16[224,1536]{1,0:T(8,128)(2,1)}) custom-call(bf16[224,1024]{1,0:T(8,128)(2,1)} %pad_maximum_fusion.att, bf16[224,5120]{1,0:T(8,128)(2,1)} %x.1, f32[1,5120]{1,0:T(1,128)} %get-tuple-element.30.gain_mlp, f32[1,5120]{1,0:T(1,128)} %get-tuple-element.44.gain_next, bf16[2,1024,5120]{2,1,0:T(8,128)(2,1)} %wo.3, ...), custom_call_target="tpu_custom_call" | custom-call | tf_op jit(solution)/shard_map/layer0/pallas_call | solution.py:319
  114.9 0.9 slice.250
  115.9 0.8 slice_convert_fusion.2
  116.7 0.9 slice_convert_fusion
  117.8 1.1 convert_bitcast_fusion
  121.2 7.9 %fusion.2 = f32[96,2,4,256]{3,2,1,0:T(4,128)S(1)} fusion(bf16[96,2,4,128]{3,2,1,0:T(4,128)(2,1)S(1)} %bitcast.183, bf16[2,97,2,256,128]{4,3,2,1,0:T(8,128)(2,1)} %param.24), kind=kOutput, calls=%fused_computation.2 | convolution fusion | flops 50331648 | bytes 13565952 | tf_op jit(solution)/shard_map/bgrd,bgsd->bgrs/dot_general | solution.py:52
  129.1 0.6 copy.106
  130.7 0.6 fusion.74
  131.9 0.8 copy.112
  132.9 6.3 %fusion.53 = bf16[96,2,4,128]{3,2,1,0:T(4,128)(2,1)S(1)} fusion(bf16[96,2,4,256]{3,2,1,0:T(4,128)(2,1)S(1)} %copy.112, bf16[2,97,2,256,128]{4,3,2,1,0:T(8,128)(2,1)} %param.25, f32[96,2,128]{2,1,0:T(2,128)S(1)} %reshape.224, f32[96,2,4]{2,1,0:T(2,128)S(1)} %copy.113), kind=kOutput, calls=%fused_computation.57 | convolution fusion | flops 50626560 | bytes 13274112 | tf_op jit(solution)/shard_map/bgrs,bgsd->bgrd/dot_general | solution.py:56
  139.3 1.3 fusion.111
  141.6 1.2 convolution_bitcast_fusion.1
  143.2 0.8 pad_maximum_fusion.1.att
  144.0 69.0 %layer1.1 = bf16[224,5120]{1,0:T(8,128)(2,1)} custom-call(bf16[224,1024]{1,0:T(8,128)(2,1)} %pad_maximum_fusion.1.att, bf16[224,5120]{1,0:T(8,128)(2,1)} %get-tuple-element.8.x, f32[1,5120]{1,0:T(1,128)} %get-tuple-element.29.gain_mlp, f32[1,5120]{1,0:T(1,128)} %get-tuple-element.44.gain_next, bf16[2,1024,5120]{2,1,0:T(8,128)(2,1)} %wo.3, ...), custom_call_target="tpu_custom_call" | custom-call | tf_op jit(solution)/shard_map/layer1/pallas_call | solution.py:319
  213.0 3.2 %copy.160 = bf16[224,5120]{1,0:T(8,128)(2,1)} copy(bf16[224,5120]{1,0:T(8,128)(2,1)} %layer1.1) | data formatting | bytes 4587520
  (91 shorter events, 11.9 us)
Async XLA Ops:
  0.0 6.4 %copy-start = (bf16[224,5120]{1,0:T(8,128)(2,1)S(1)}, bf16[224,5120]{1,0:T(8,128)(2,1)}, u32[]{:S(2)}) copy-start(bf16[224,5120]{1,0:T(8,128)(2,1)} %x.1) | copy-start | bytes 6881284
  0.0 5.7 %copy-start.13 = (s32[97]{0:T(128)S(1)}, s32[97]{0:T(128)}, u32[]{:S(2)}) copy-start(s32[97]{0:T(128)} %param.14) | copy-start | bytes 1168
  0.0 5.7 %copy-start.9 = (bf16[2,5120]{1,0:T(2,128)(2,1)S(1)}, bf16[2,5120]{1,0:T(2,128)(2,1)}, u32[]{:S(2)}) copy-start(bf16[2,5120]{1,0:T(2,128)(2,1)} %param.20) | copy-start | bytes 61444
  0.0 5.7 %copy-start.10 = (bf16[2,5120]{1,0:T(2,128)(2,1)S(1)}, bf16[2,5120]{1,0:T(2,128)(2,1)}, u32[]{:S(2)}) copy-start(bf16[2,5120]{1,0:T(2,128)(2,1)} %param.15) | copy-start | bytes 61444
  2.1 36.2 %copy-start.11 = (pred[256]{0:T(512)(128)(4,1)}, pred[256]{0:T(512)(128)(4,1)S(1)}, u32[]{:S(2)}) copy-start(pred[256]{0:T(512)(128)(4,1)S(1)} %iota_compare_fusion.2) | copy-start | bytes 772
  5.7 14.3 %copy-start.7 = (pred[128,128]{1,0:T(8,128)(4,1)}, pred[128,128]{1,0:T(8,128)(4,1)S(1)}, u32[]{:S(2)}) copy-start(pred[128,128]{1,0:T(8,128)(4,1)S(1)} %iota_compare_fusion.1) | copy-start | bytes 49156
  5.8 23.2 %copy-start.5 = (pred[96,256]{0,1:T(8,128)(4,1)}, pred[96,256]{0,1:T(8,128)(4,1)S(1)}, u32[]{:S(2)}) copy-start(pred[96,256]{0,1:T(8,128)(4,1)S(1)} %iota_compare_fusion) | copy-start | bytes 73732
  9.7 9.1 %copy-start.1 = (f32[224,64]{1,0:T(8,128)}, f32[224,64]{1,0:T(8,128)S(1)}, u32[]{:S(2)}) copy-start(f32[224,64]{1,0:T(8,128)S(1)} %get-tuple-element.33) | copy-start | bytes 172036
  9.7 9.1 %copy-start.3 = (f32[224,64]{1,0:T(8,128)}, f32[224,64]{1,0:T(8,128)S(1)}, u32[]{:S(2)}) copy-start(f32[224,64]{1,0:T(8,128)S(1)} %get-tuple-element.34) | copy-start | bytes 172036
  114.8 4.2 %copy-start.2 = (f32[224,64]{1,0:T(8,128)S(1)}, f32[224,64]{1,0:T(8,128)}, u32[]{:S(2)}) copy-start(f32[224,64]{1,0:T(8,128)} %copy-done.1) | copy-start | bytes 172036
  114.9 4.2 %copy-start.4 = (f32[224,64]{1,0:T(8,128)S(1)}, f32[224,64]{1,0:T(8,128)}, u32[]{:S(2)}) copy-start(f32[224,64]{1,0:T(8,128)} %copy-done.3) | copy-start | bytes 172036
  119.7 1.0 copy-start.8
  121.2 8.5 %copy-start.6 = (pred[96,256]{0,1:T(8,128)(4,1)S(1)}, pred[96,256]{0,1:T(8,128)(4,1)}, u32[]{:S(2)}) copy-start(pred[96,256]{0,1:T(8,128)(4,1)} %copy-done.5) | copy-start | bytes 73732
  132.8 6.5 %copy-start.12 = (pred[256]{0:T(512)(128)(4,1)S(1)}, pred[256]{0:T(512)(128)(4,1)}, u32[]{:S(2)}) copy-start(pred[256]{0:T(512)(128)(4,1)} %copy-done.11) | copy-start | bytes 772

commit v2 on v0

v2 whole, which is shorter than its diff:
```python
import functools

import jax
import jax.numpy as jnp
from jax import lax
from jax.experimental import pallas as pl
from jax.experimental.pallas import tpu as pltpu
from jax.sharding import PartitionSpec as P

ROPE_BASE = 500000.0
EPSILON = 1e-5
MESH = pl.DeviceIdType.MESH
F32 = jnp.float32
BF16 = jnp.bfloat16
CW = 512
G_SLOTS = 3
D_SLOTS = 4
KV_SLOTS = 3
KV_ROWS = 8
O, M = 0, 1
DEC, PRE = 0, 1


def step_kernel(dims, lens, x_in, cos, sin, gain_a, gain_m, wq, wk, wv, wo, wg, wu, wd, kc, vc, y,
                gbuf, dbuf, acc, act, pbuf, rbuf, xb_o, xb_m, h_o, h_m, ssq, pre, kbuf, vbuf, kpre, vpre,
                qs, kn, vn, qp, kp, vp, att,
                q_sem, w_sem, k_sem, v_sem, g_sem, d_sem, kv_sem, kvp_sem, y_sem, p_ss, p_rs, x_ss, x_rs, h_ss, h_rs):
    dec, chunk = dims
    rows = dec + chunk
    width = x_in.shape[1]
    layers, o_depth = wo.shape[0], wo.shape[1]
    ff = wg.shape[2]
    q_cols, k_cols = wq.shape[2], wk.shape[2]
    n_qkv = q_cols + 2 * k_cols
    seq, hd = kc.shape[3], kc.shape[4]
    heads, kv_heads = q_cols // hd, k_cols // hd
    group = heads // kv_heads
    n_chunks = width // CW
    o_per_slot = ff // o_depth
    scale_qk = hd ** -0.5
    base = (0, dec)
    size = (dec, chunk)
    half = (dec // 2, chunk // 2)
    rbase = (0, dec // 2)

    dp_me = lax.axis_index('dp')
    me = lax.axis_index('tp')
    core = lax.rem(me, 2)
    core_peer = (dp_me, me + 1 - 2 * core)
    x_peer = (dp_me, lax.rem(me + 2, 4))

    def own(part):
        return pl.ds(pl.multiple_of(base[part] + core * half[part], 16), half[part])

    def oth(part):
        return pl.ds(pl.multiple_of(base[part] + (1 - core) * half[part], 16), half[part])

    def whole(part):
        return pl.ds(base[part], size[part])

    def landed(part):
        return pl.ds(rbase[part], half[part])

    def cols(j):
        return pl.ds(pl.multiple_of(j * CW, CW), CW)

    xbs = (xb_o, xb_m)
    hs = (h_o, h_m)

    def x_load(j):
        return pltpu.make_async_copy(x_in.at[:, cols(j)], h_m.at[j], y_sem.at[0, j])

    def wo_copy(l, j):
        return pltpu.make_async_copy(wo.at[l, :, cols(j)], dbuf.at[j // o_per_slot, pl.ds(pl.multiple_of(lax.rem(j, o_per_slot) * o_depth, 16), o_depth), :], w_sem.at[j])

    def g_copies(l, j):
        slot = lax.rem(j, G_SLOTS)
        return (pltpu.make_async_copy(wg.at[l, cols(j), :], gbuf.at[slot, 0], g_sem.at[slot, 0]),
                pltpu.make_async_copy(wu.at[l, cols(j), :], gbuf.at[slot, 1], g_sem.at[slot, 1]))

    def d_copy(l, j):
        slot = lax.rem(j, D_SLOTS)
        return pltpu.make_async_copy(wd.at[l, :, cols(j)], dbuf.at[slot], d_sem.at[slot])

    def qkv_place(j):
        return j // 4, lax.rem(j // 2, 2), lax.rem(j, 2) * (ff // 2)

    def qkv_copies(l, j):
        slot, which, left = qkv_place(j)
        dst = gbuf.at[slot, which]

        def at(off, n):
            return dst.at[:, pl.ds(pl.multiple_of(left + off, 128), n)]

        return (pltpu.make_async_copy(wq.at[l, cols(j), :], at(0, q_cols), q_sem.at[j]),
                pltpu.make_async_copy(wk.at[l, cols(j), :], at(q_cols, k_cols), k_sem.at[j]),
                pltpu.make_async_copy(wv.at[l, cols(j), :], at(q_cols + k_cols, k_cols), v_sem.at[j]))

    def kv_copies(l, i):
        slot = lax.rem(i, KV_SLOTS)
        src = pl.ds(i * KV_ROWS, KV_ROWS)
        return (pltpu.make_async_copy(kc.at[l, src], kbuf.at[slot], kv_sem.at[slot, 0]),
                pltpu.make_async_copy(vc.at[l, src], vbuf.at[slot], kv_sem.at[slot, 1]))

    def kv_pre_copies(l):
        return (pltpu.make_async_copy(kc.at[l, dec], kpre, kvp_sem.at[0]),
                pltpu.make_async_copy(vc.at[l, dec], vpre, kvp_sem.at[1]))

    def start(copies):
        for c in copies:
            c.start()

    def wait(copies):
        for c in copies:
            c.wait()

    def p_copy(ar, part, j):
        return pltpu.make_async_remote_copy(pbuf.at[j, oth(part), :], rbuf.at[j, landed(part), :], p_ss.at[ar, part, j], p_rs.at[ar, part, j], device_id=core_peer, device_id_type=MESH)

    def x_copy(ar, part, j):
        return pltpu.make_async_remote_copy(pbuf.at[j, own(part), :], xbs[ar].at[j, landed(part), :], x_ss.at[ar, part, j], x_rs.at[ar, part, j], device_id=x_peer, device_id_type=MESH)

    def h_copy(ar, part, j):
        return pltpu.make_async_remote_copy(hs[ar].at[j, own(part), :], hs[ar].at[j, own(part), :], h_ss.at[ar, part, j], h_rs.at[ar, part, j], device_id=core_peer, device_id_type=MESH)

    def h_wait(ar, part, j):
        pltpu.make_async_remote_copy(hs[ar].at[j, oth(part), :], hs[ar].at[j, oth(part), :], h_ss.at[ar, part, j], h_rs.at[ar, part, j], device_id=core_peer, device_id_type=MESH).wait_recv()

    def sent(l, ar, part, j):
        if l > 0 or ar == M:
            p_copy(1 - ar, part, j).wait_send()
            x_copy(1 - ar, part, j).wait_send()

    def pair_sum(ar, part, j):
        p_copy(ar, part, j).wait_recv()
        pbuf[j, own(part), :] = (pbuf[j, own(part), :].astype(F32) + rbuf[j, landed(part), :].astype(F32)).astype(BF16)
        x_copy(ar, part, j).start()

    def finish(l, ar, part, j):
        x_copy(ar, part, j).wait_recv()
        total = pbuf[j, own(part), :].astype(F32) + xbs[ar][j, landed(part), :].astype(F32)
        resid = hs[1 - ar][j, own(part), :].astype(F32)
        if l > 0:
            h_copy(ar, part, j).wait_send()
        hs[ar][j, own(part), :] = (resid + total).astype(BF16)
        h_copy(ar, part, j).start()

    def add_squares(r, vals):
        sq = vals * vals
        ssq[r, :] += sq[:, :128] + sq[:, 128:256] + sq[:, 256:384] + sq[:, 384:]

    def inv_rms(r):
        return lax.rsqrt(jnp.sum(ssq[r, :], axis=-1, keepdims=True) * (1.0 / width) + EPSILON)

    def next_scale(r):
        inv = inv_rms(r)
        scale = inv / pre[r, :1]
        n = ssq[r, :].shape[0]
        pre[r, :] = jnp.broadcast_to(jnp.maximum(inv, 1e-30), (n, 128))
        ssq[r, :] = jnp.zeros((n, 128), F32)
        return scale

    def qkv_block(l, part, j):
        r = whole(part)
        if l > 0:
            h_wait(M, part, j)
        vals = h_m[j, r, :].astype(F32)
        add_squares(r, vals)
        a = (vals * pre[r, :1] * gain_a[l:l + 1, cols(j)]).astype(BF16)
        if part == DEC:
            wait(qkv_copies(l, j))
        slot, which, left = qkv_place(j)
        for n in range(n_qkv // CW):
            acc[r, n * CW:(n + 1) * CW] += jnp.dot(a, gbuf[slot, which, :, pl.ds(pl.multiple_of(left + n * CW, 128), CW)], preferred_element_type=F32)

    def qkv_part(l, part):
        r = whole(part)
        acc[r, :n_qkv] = jnp.zeros((size[part], n_qkv), F32)

        def step(j, c):
            if l > 0:
                finish(l - 1, M, part, j)

                @pl.when(j >= 1)
                def _():
                    qkv_block(l, part, j - 1)
            else:
                qkv_block(l, part, j)
            return c

        lax.fori_loop(0, n_chunks, step, 0)
        if l > 0:
            qkv_block(l, part, n_chunks - 1)
        scale = next_scale(r)
        c_tab, s_tab = cos[r, :], sin[r, :]

        def head(col):
            return (acc[r, col * hd:(col + 1) * hd] * scale).astype(BF16).astype(F32)

        def rope(t):
            return (t * c_tab + pltpu.roll(t, hd // 2, 1) * s_tab).astype(BF16)

        for h in range(heads):
            q = rope(head(h))
            if part == DEC:
                qs[pl.ds(h, dec, stride=heads), :] = q.astype(F32)
            else:
                qp[:, h * hd:(h + 1) * hd] = q
        for g in range(kv_heads):
            k = rope(head(heads + g))
            v = head(heads + kv_heads + g)
            if part == DEC:
                for h in range(g * group, (g + 1) * group):
                    kn[pl.ds(h, dec, stride=heads), :] = k.astype(F32)
                    vn[pl.ds(h, dec, stride=heads), :] = v
            else:
                kp[:, g * hd:(g + 1) * hd] = k
                vp[:, g * hd:(g + 1) * hd] = v.astype(BF16)

    def decode_attention(l):
        first_rows = lax.broadcasted_iota(jnp.int32, (heads, hd), 0) < group
        places = lax.broadcasted_iota(jnp.int32, (heads, seq), 1)
        n_blocks = dec // KV_ROWS

        def block(i, c):
            wait(kv_copies(l, i))
            slot = lax.rem(i, KV_SLOTS)
            for n in range(KV_ROWS):
                b = i * KV_ROWS + n
                r = pl.ds(pl.multiple_of(b * heads, heads), heads)
                q = qs[r, :]
                zero = jnp.zeros_like(q)
                q2 = jnp.concatenate([jnp.where(first_rows, q, zero), jnp.where(first_rows, zero, q)], axis=1).astype(BF16)
                k2 = jnp.concatenate([kbuf[slot, n, 0], kbuf[slot, n, 1]], axis=1)
                v2 = jnp.concatenate([vbuf[slot, n, 0], vbuf[slot, n, 1]], axis=1)
                s = lax.dot_general(q2, k2, (((1,), (1,)), ((), ())), preferred_element_type=F32) * scale_qk
                s = jnp.where(places < lens[b], s, -jnp.inf)
                s_new = jnp.sum(q * kn[r, :], axis=-1, keepdims=True) * scale_qk
                top = jnp.maximum(jnp.max(s, axis=-1, keepdims=True), s_new)
                e = jnp.exp(s - top)
                e_new = jnp.exp(s_new - top)
                inv = 1.0 / (jnp.sum(e, axis=-1, keepdims=True) + e_new)
                o = jnp.dot((e * inv).astype(BF16), v2, preferred_element_type=F32)
                qs[r, :] = jnp.where(first_rows, o[:, :hd], o[:, hd:]) + (e_new * inv).astype(BF16).astype(F32) * vn[r, :]

            @pl.when(i + KV_SLOTS < n_blocks)
            def _():
                start(kv_copies(l, i + KV_SLOTS))
            return c

        lax.fori_loop(0, n_blocks, block, 0)
        for h in range(heads):
            att[:dec, h * hd:(h + 1) * hd] = qs[pl.ds(h, dec, stride=heads), :].astype(BF16)

    def prefill_attention(l):
        wait(kv_pre_copies(l))
        n_old = lens[dec]
        old = lax.broadcasted_iota(jnp.int32, (chunk, seq), 1) < n_old
        causal = lax.broadcasted_iota(jnp.int32, (chunk, chunk), 1) <= lax.broadcasted_iota(jnp.int32, (chunk, chunk), 0)

        def heads_step(i, c):
            for g in range(kv_heads):
                col = pl.ds(pl.multiple_of((g * group + i) * hd, hd), hd)
                q = qp[:, col]
                kv_col = slice(g * hd, (g + 1) * hd)
                s = lax.dot_general(q, kpre[g], (((1,), (1,)), ((), ())), preferred_element_type=F32) * scale_qk
                s = jnp.where(old, s, -jnp.inf)
                t = lax.dot_general(q, kp[:, kv_col], (((1,), (1,)), ((), ())), preferred_element_type=F32) * scale_qk
                t = jnp.where(causal, t, -jnp.inf)
                top = jnp.maximum(jnp.max(s, axis=-1, keepdims=True), jnp.max(t, axis=-1, keepdims=True))
                es = jnp.exp(s - top)
                et = jnp.exp(t - top)
                inv = 1.0 / (jnp.sum(es, axis=-1, keepdims=True) + jnp.sum(et, axis=-1, keepdims=True))
                o = jnp.dot((es * inv).astype(BF16), vpre[g], preferred_element_type=F32)
                o += jnp.dot((et * inv).astype(BF16), vp[:, kv_col], preferred_element_type=F32)
                att[pl.ds(dec, chunk), col] = o.astype(BF16)
            return c

        lax.fori_loop(0, group, heads_step, 0)

    def o_part(l, part):
        r = whole(part)

        def step(j, c):
            if part == DEC:
                wo_copy(l, j).wait()
            w = dbuf[j // o_per_slot, pl.ds(pl.multiple_of(lax.rem(j, o_per_slot) * o_depth, 16), o_depth), :]
            sent(l, O, part, j)
            pbuf[j, r, :] = jnp.dot(att[r, :], w, preferred_element_type=F32).astype(BF16)
            p_copy(O, part, j).start()

            @pl.when(j >= 1)
            def _():
                pair_sum(O, part, j - 1)
            return c

        lax.fori_loop(0, n_chunks, step, 0)
        pair_sum(O, part, n_chunks - 1)

    def gate_up(l):
        def block(j):
            h_wait(O, DEC, j)
            h_wait(O, PRE, j)
            vals = h_o[j].astype(F32)
            add_squares(pl.ds(0, rows), vals)
            a = (vals * pre[:, :1] * gain_m[l:l + 1, cols(j)]).astype(BF16)
            slot = lax.rem(j, G_SLOTS)
            wait(g_copies(l, j))

            def mat(m, c):
                for n in range(ff // CW):
                    col = pl.ds(pl.multiple_of(m * ff + n * CW, CW), CW)
                    acc[:, col] += jnp.dot(a, gbuf[slot, m, :, n * CW:(n + 1) * CW], preferred_element_type=F32)
                return c

            lax.fori_loop(0, 2, mat, 0)

            @pl.when(j + G_SLOTS < n_chunks)
            def _():
                start(g_copies(l, j + G_SLOTS))

            @pl.when(j >= n_chunks - D_SLOTS)
            def _():
                d_copy(l, j - (n_chunks - D_SLOTS)).start()

        def step(j, c):
            finish(l, O, DEC, j)
            finish(l, O, PRE, j)

            @pl.when(j >= 1)
            def _():
                block(j - 1)
            return c

        lax.fori_loop(0, n_chunks, step, 0)
        block(n_chunks - 1)
        scale = next_scale(pl.ds(0, rows))

        def act_step(n, c):
            gate = acc[:, cols(n)] * scale
            up = acc[:, pl.ds(pl.multiple_of(ff + n * CW, CW), CW)] * scale
            act[:, cols(n)] = (gate * jax.nn.sigmoid(gate) * up).astype(BF16)
            return c

        lax.fori_loop(0, ff // CW, act_step, 0)

    def down(l):
        def step(j, c):
            d_copy(l, j).wait()
            for part in (DEC, PRE):
                sent(l, M, part, j)
            pbuf[j] = jnp.dot(act[...], dbuf[lax.rem(j, D_SLOTS)], preferred_element_type=F32).astype(BF16)
            for part in (DEC, PRE):
                p_copy(M, part, j).start()

            @pl.when(j + D_SLOTS < n_chunks)
            def _():
                d_copy(l, j + D_SLOTS).start()

            if l + 1 < layers:
                start(qkv_copies(l + 1, j))

            @pl.when(j >= 1)
            def _():
                pair_sum(M, DEC, j - 1)
            return c

        lax.fori_loop(0, n_chunks, step, 0)
        pair_sum(M, DEC, n_chunks - 1)
        if l + 1 < layers:
            start(kv_pre_copies(l + 1))
            for i in range(KV_SLOTS):
                start(kv_copies(l + 1, i))
            for j in range(n_chunks):
                wo_copy(l + 1, j).start()

        def pre_step(j, c):
            pair_sum(M, PRE, j)
            return c

        lax.fori_loop(0, n_chunks, pre_step, 0)

    for j in range(n_chunks):
        x_load(j).start()
    barrier = pltpu.get_barrier_semaphore()
    for peer in (core_peer, x_peer):
        pl.semaphore_signal(barrier, inc=1, device_id=peer, device_id_type=MESH)
    ssq[...] = jnp.zeros_like(ssq)
    for j in range(n_chunks):
        start(qkv_copies(0, j))
    for i in range(KV_SLOTS):
        start(kv_copies(0, i))
    for j in range(n_chunks):
        wo_copy(0, j).start()
    start(kv_pre_copies(0))
    for j in range(n_chunks):
        x_load(j).wait()

    def sq_step(j, c):
        add_squares(pl.ds(0, rows), h_m[j].astype(F32))
        return c

    lax.fori_loop(0, n_chunks, sq_step, 0)
    pre[...] = jnp.broadcast_to(jnp.maximum(inv_rms(pl.ds(0, rows)), 1e-30), pre.shape)
    ssq[...] = jnp.zeros_like(ssq)
    pl.semaphore_wait(barrier, 2)

    for l in range(layers):
        qkv_part(l, DEC)
        decode_attention(l)
        o_part(l, DEC)
        qkv_part(l, PRE)
        for j in range(G_SLOTS):
            start(g_copies(l, j))
        prefill_attention(l)
        o_part(l, PRE)
        acc[...] = jnp.zeros_like(acc)
        gate_up(l)
        down(l)

    def out_copy(part, j):
        r = whole(part)
        return pltpu.make_async_copy(h_m.at[j, r, :], y.at[r, cols(j)], y_sem.at[part, j])

    for part in (DEC, PRE):
        def out_step(j, c):
            finish(layers - 1, M, part, j)

            @pl.when(j >= 1)
            def _():
                h_wait(M, part, j - 1)
                out_copy(part, j - 1).start()
            return c

        lax.fori_loop(0, n_chunks, out_step, 0)
        h_wait(M, part, n_chunks - 1)
        out_copy(part, n_chunks - 1).start()
    for part in (DEC, PRE):
        for j in range(n_chunks):
            out_copy(part, j).wait()
            h_copy(O, part, j).wait_send()
            h_copy(M, part, j).wait_send()
            p_copy(M, part, j).wait_send()
            x_copy(M, part, j).wait_send()


def step_call(lengths, x, cos_tab, sin_tab, attn_gain, mlp_gain, w_q, w_k, w_v, w_o, w_gate, w_up, w_down, k_cache, v_cache):
    rows, width = x.shape
    dec = lengths.shape[0] - 1
    chunk = rows - dec
    ff = w_gate.shape[2]
    n_chunks = width // CW
    q_cols, k_cols = w_q.shape[2], w_k.shape[2]
    kv_heads, seq, hd = k_cache.shape[2:]
    heads = q_cols // hd
    vmem = pl.BlockSpec(memory_space=pltpu.VMEM)
    hbm = pl.BlockSpec(memory_space=pl.ANY)
    smem = pl.BlockSpec(memory_space=pltpu.SMEM)
    sem = pltpu.SemaphoreType.DMA
    buf = pltpu.VMEM
    return pl.pallas_call(
        functools.partial(step_kernel, (dec, chunk)),
        out_shape=jax.ShapeDtypeStruct((rows, width), BF16),
        in_specs=[smem, hbm, vmem, vmem, vmem, vmem] + [hbm] * 9,
        out_specs=hbm,
        scratch_shapes=[
            buf((G_SLOTS, 2, CW, ff), BF16),
            buf((D_SLOTS, ff, CW), BF16),
            buf((rows, 2 * ff), F32),
            buf((rows, ff), BF16),
            buf((n_chunks, rows, CW), BF16),
            buf((n_chunks, rows // 2, CW), BF16),
            buf((n_chunks, rows // 2, CW), BF16),
            buf((n_chunks, rows // 2, CW), BF16),
            buf((n_chunks, rows, CW), BF16),
            buf((n_chunks, rows, CW), BF16),
            buf((rows, 128), F32),
            buf((rows, 128), F32),
            buf((KV_SLOTS, KV_ROWS, kv_heads, seq, hd), BF16),
            buf((KV_SLOTS, KV_ROWS, kv_heads, seq, hd), BF16),
            buf((kv_heads, seq, hd), BF16),
            buf((kv_heads, seq, hd), BF16),
            buf((dec * heads, hd), F32),
            buf((dec * heads, hd), F32),
            buf((dec * heads, hd), F32),
            buf((chunk, q_cols), BF16),
            buf((chunk, k_cols), BF16),
            buf((chunk, k_cols), BF16),
            buf((rows, q_cols), BF16),
            sem((n_chunks,)),
            sem((n_chunks,)),
            sem((n_chunks,)),
            sem((n_chunks,)),
            sem((G_SLOTS, 2)),
            sem((D_SLOTS,)),
            sem((KV_SLOTS, 2)),
            sem((2,)),
            sem((2, n_chunks)),
            sem((2, 2, n_chunks)),
            sem((2, 2, n_chunks)),
            sem((2, 2, n_chunks)),
            sem((2, 2, n_chunks)),
            sem((2, 2, n_chunks)),
            sem((2, 2, n_chunks)),
        ],
        compiler_params=pltpu.CompilerParams(collective_id=0, has_side_effects=True, vmem_limit_bytes=67043328),
        name='decoder_step',
    )(lengths, x, cos_tab, sin_tab, attn_gain, mlp_gain, w_q, w_k, w_v, w_o, w_gate, w_up, w_down, k_cache, v_cache)


def solution(mesh):
    col_spec = P(None, None, 'tp')
    row_spec = P(None, 'tp', None)
    cache_spec = P(None, 'dp', 'tp', None, None)
    in_specs = (P('dp', None), P('dp'), P(), col_spec, col_spec, col_spec, row_spec, P(), col_spec, col_spec, row_spec, cache_spec, cache_spec)

    def body(x, lengths, attn_gain, w_q, w_k, w_v, w_o, mlp_gain, w_gate, w_up, w_down, k_cache, v_cache):
        dec_rows = lengths.shape[0] - 1
        chunk_len = x.shape[0] - dec_rows
        head_dim = k_cache.shape[-1]
        positions = jnp.concatenate([lengths[:dec_rows], lengths[dec_rows] + jnp.arange(chunk_len, dtype=jnp.int32)])
        freq_exps = jnp.arange(0, head_dim, 2, dtype=F32) / head_dim
        angles = positions.astype(F32)[:, None] * jnp.power(ROPE_BASE, -freq_exps)[None, :]
        cos_tab, sin_tab = jnp.cos(angles), jnp.sin(angles)
        cos_tab = jnp.concatenate([cos_tab, cos_tab], axis=-1)
        sin_tab = jnp.concatenate([-sin_tab, sin_tab], axis=-1)
        return step_call(lengths, x, cos_tab, sin_tab, attn_gain.astype(F32), mlp_gain.astype(F32), w_q, w_k, w_v, w_o, w_gate, w_up, w_down, k_cache, v_cache)

    return jax.shard_map(body, mesh=mesh, in_specs=in_specs, out_specs=P('dp', None), check_vma=False)
```

time: 451 us -> 247 us (0.55); the launches traced: 443 us -> 247 us
  Pallas kernels: 0 us -> 237 us
  waiting for transfers between devices: 198 us -> 0 us
  matrix products: 175 us -> 0 us
  other arithmetic: 35.9 us -> 5.37 us
  local copies, waits for them, and re-layouts: 18.9 us -> 4.41 us
  between operations: 14.2 us -> 0.03 us
    pallas_call x0 -> x1, Pallas kernels: none -> 237 us  [step_call(): pl.pallas_call(functools.partial(step_kernel, (dec, chunk)), out_shape=ja...]
    psum x4 -> x0, waiting for transfers between devices: 198 us -> none  [the longest x2 100 us: decoder_layer(): attn_sum = lax.psum(attn_part, 'tp')]
    dot_general x28 -> x0, matrix products: 175 us -> none  [the longest x2 34 us: decoder_layer(): jnp.dot(activated, w_down, preferred_element_type=jnp.float32)]
    reduce_sum x8 -> x0, other arithmetic: 15.9 us -> none  [the longest x4 11.9 us: rms_norm(): jnp.mean(x_f32 * x_f32, axis=-1, keepdims=True) + EPSILON]
    slice x13 -> x0, local copies, waits for them, and re-layouts: 6.7 us -> none  [the longest x4 4.3 us: attention(): dec_prob[..., :seq_len]]
    convert_element_type x9 -> x3, other arithmetic: 8.98 us -> 3.43 us  [the longest x1 1.36 us: body(): attn_gain.astype(F32)]
  transfers between devices with their start and end apart: 4 -> 0, of which waited for: 4 -> 0; matrix products, arithmetic and copies ran while one was open for 0% -> 0% of each run, Pallas kernels for 0% -> 0%
where the time goes in v2:
time: 247 us
  Pallas kernels  237 us (96%)
  other arithmetic  5.37 us (2%)
  local copies, waits for them, and re-layouts  4.41 us (2%)
    pallas_call x1, Pallas kernels, step_call(): pl.pallas_call(functools.partial(step_kernel, (dec, chunk)), out_shape=ja...  237 us

profile of v2, /device:TPU:0, one launch (start us, length us, event | category | flops | bytes accessed | tf_op | source)
XLA Modules:
  0.0 247.2 jit_solution(8340114910398650738)
XLA Ops:
  0.0 1.2 slice.7
  1.2 0.6 iota_add_fusion
  1.9 0.7 add_convert_fusion
  2.6 1.4 convert_element_type.14.gain_a
  4.0 1.3 convert_element_type.15.gain_m
  5.3 0.5 fusion
  5.8 0.8 pad_maximum_fusion
  6.6 237.4 %decoder_step.1 = bf16[224,5120]{1,0:T(8,128)(2,1)} custom-call(s32[97]{0:T(128)} %lens.1, bf16[224,5120]{1,0:T(8,128)(2,1)} %x_in.1, f32[224,128]{1,0:T(8,128)} %get-tuple-element.8.cos, f32[224,128]{1,0:T(8,128)} %get-tuple-element.9.sin, f32[2,5120]{1,0:T(2,128)} %convert_element_type.14.gain_a, f32[2,5120]{1,0:T(2,128)} %convert_element_type.15.gain_m, ...), custom_call_target="tpu_custom_call" | custom-call | tf_op jit(solution)/shard_map/decoder_step/pallas_call | solution.py:461
  244.0 3.2 %copy.15 = bf16[224,5120]{1,0:T(8,128)(2,1)} copy(bf16[224,5120]{1,0:T(8,128)(2,1)} %decoder_step.1) | data formatting | bytes 4587520
  (1 shorter events, 0.0 us)

commit v3 on v2

--- a/solution.py
+++ b/solution.py
@@ -2,6 +2,7 @@
 
 import jax
 import jax.numpy as jnp
+import numpy as np
 from jax import lax
 from jax.experimental import pallas as pl
 from jax.experimental.pallas import tpu as pltpu
@@ -13,16 +14,16 @@
 F32 = jnp.float32
 BF16 = jnp.bfloat16
 CW = 512
-G_SLOTS = 3
+G_SLOTS = 5
 D_SLOTS = 4
-KV_SLOTS = 3
-KV_ROWS = 8
+KV_SLOTS = 2
+KV_ROWS = 16
 O, M = 0, 1
 DEC, PRE = 0, 1
 
 
-def step_kernel(dims, lens, x_in, cos, sin, gain_a, gain_m, wq, wk, wv, wo, wg, wu, wd, kc, vc, y,
-                gbuf, dbuf, acc, act, pbuf, rbuf, xb_o, xb_m, h_o, h_m, ssq, pre, kbuf, vbuf, kpre, vpre,
+def step_kernel(dims, lens, x_in, freq, gain_a, gain_m, wq, wk, wv, wo, wg, wu, wd, kc, vc, y,
+                gbuf, dbuf, acc, act, pbuf, rbuf, xb_o, xb_m, h_o, h_m, ssq, pre, cos, sin, kbuf, vbuf, kpre, vpre,
                 qs, kn, vn, qp, kp, vp, att,
                 q_sem, w_sem, k_sem, v_sem, g_sem, d_sem, kv_sem, kvp_sem, y_sem, p_ss, p_rs, x_ss, x_rs, h_ss, h_rs):
     dec, chunk = dims
@@ -73,21 +74,20 @@
     def wo_copy(l, j):
         return pltpu.make_async_copy(wo.at[l, :, cols(j)], dbuf.at[j // o_per_slot, pl.ds(pl.multiple_of(lax.rem(j, o_per_slot) * o_depth, 16), o_depth), :], w_sem.at[j])
 
-    def g_copies(l, j):
-        slot = lax.rem(j, G_SLOTS)
-        return (pltpu.make_async_copy(wg.at[l, cols(j), :], gbuf.at[slot, 0], g_sem.at[slot, 0]),
-                pltpu.make_async_copy(wu.at[l, cols(j), :], gbuf.at[slot, 1], g_sem.at[slot, 1]))
+    def g_copy(l, j, m):
+        slot = lax.rem(2 * j + m, G_SLOTS)
+        return pltpu.make_async_copy((wg, wu)[m].at[l, cols(j), :], gbuf.at[slot], g_sem.at[slot])
 
     def d_copy(l, j):
         slot = lax.rem(j, D_SLOTS)
         return pltpu.make_async_copy(wd.at[l, :, cols(j)], dbuf.at[slot], d_sem.at[slot])
 
     def qkv_place(j):
-        return j // 4, lax.rem(j // 2, 2), lax.rem(j, 2) * (ff // 2)
+        return j // 2, lax.rem(j, 2) * (ff // 2)
 
     def qkv_copies(l, j):
-        slot, which, left = qkv_place(j)
-        dst = gbuf.at[slot, which]
+        slot, left = qkv_place(j)
+        dst = gbuf.at[slot]
 
         def at(off, n):
             return dst.at[:, pl.ds(pl.multiple_of(left + off, 128), n)]
@@ -160,37 +160,47 @@
         ssq[r, :] = jnp.zeros((n, 128), F32)
         return scale
 
-    def qkv_block(l, part, j):
+    def qkv_block(l, part, pair):
         r = whole(part)
-        if l > 0:
-            h_wait(M, part, j)
-        vals = h_m[j, r, :].astype(F32)
-        add_squares(r, vals)
-        a = (vals * pre[r, :1] * gain_a[l:l + 1, cols(j)]).astype(BF16)
-        if part == DEC:
-            wait(qkv_copies(l, j))
-        slot, which, left = qkv_place(j)
+        a = []
+        for j in pair:
+            if l > 0:
+                h_wait(M, part, j)
+            vals = h_m[j, r, :].astype(F32)
+            add_squares(r, vals)
+            a.append((vals * pre[r, :1] * gain_a[l:l + 1, cols(j)].astype(F32)).astype(BF16))
+            if part == DEC:
+                wait(qkv_copies(l, j))
         for n in range(n_qkv // CW):
-            acc[r, n * CW:(n + 1) * CW] += jnp.dot(a, gbuf[slot, which, :, pl.ds(pl.multiple_of(left + n * CW, 128), CW)], preferred_element_type=F32)
+            total = acc[r, n * CW:(n + 1) * CW]
+            for j, a_j in zip(pair, a):
+                slot, left = qkv_place(j)
+                total += jnp.dot(a_j, gbuf[slot, :, pl.ds(pl.multiple_of(left + n * CW, 128), CW)], preferred_element_type=F32)
+            acc[r, n * CW:(n + 1) * CW] = total
 
     def qkv_part(l, part):
         r = whole(part)
         acc[r, :n_qkv] = jnp.zeros((size[part], n_qkv), F32)
-
-        def step(j, c):
-            if l > 0:
-                finish(l - 1, M, part, j)
-
-                @pl.when(j >= 1)
+        n_pairs = n_chunks // 2
+
+        def pair_of(i):
+            return 2 * i, 2 * i + 1
+
+        def step(i, c):
+            if l > 0 and part == DEC:
+                for j in pair_of(i):
+                    finish(l - 1, M, part, j)
+
+                @pl.when(i >= 1)
                 def _():
-                    qkv_block(l, part, j - 1)
+                    qkv_block(l, part, pair_of(i - 1))
             else:
-                qkv_block(l, part, j)
-            return c
-
-        lax.fori_loop(0, n_chunks, step, 0)
-        if l > 0:
-            qkv_block(l, part, n_chunks - 1)
+                qkv_block(l, part, pair_of(i))
+            return c
+
+        lax.fori_loop(0, n_pairs, step, 0)
+        if l > 0 and part == DEC:
+            qkv_block(l, part, pair_of(n_pairs - 1))
         scale = next_scale(r)
         c_tab, s_tab = cos[r, :], sin[r, :]
 
@@ -225,23 +235,35 @@
         def block(i, c):
             wait(kv_copies(l, i))
             slot = lax.rem(i, KV_SLOTS)
+            if l == 0:
+                @pl.when(i == n_blocks - KV_SLOTS)
+                def _():
+                    for j in range(n_chunks):
+                        wo_copy(l, j).start()
+            scores = []
             for n in range(KV_ROWS):
                 b = i * KV_ROWS + n
-                r = pl.ds(pl.multiple_of(b * heads, heads), heads)
-                q = qs[r, :]
+                q = qs[pl.ds(pl.multiple_of(b * heads, heads), heads), :]
                 zero = jnp.zeros_like(q)
                 q2 = jnp.concatenate([jnp.where(first_rows, q, zero), jnp.where(first_rows, zero, q)], axis=1).astype(BF16)
                 k2 = jnp.concatenate([kbuf[slot, n, 0], kbuf[slot, n, 1]], axis=1)
+                s = lax.dot_general(q2, k2, (((1,), (1,)), ((), ())), preferred_element_type=F32) * scale_qk
+                scores.append(jnp.where(places < lens[b], s, -jnp.inf))
+            r = pl.ds(pl.multiple_of(i * KV_ROWS * heads, KV_ROWS * heads), KV_ROWS * heads)
+            s = jnp.concatenate(scores, axis=0)
+            s_new = jnp.sum(qs[r, :] * kn[r, :], axis=-1, keepdims=True) * scale_qk
+            top = jnp.maximum(jnp.max(s, axis=-1, keepdims=True), s_new)
+            e = jnp.exp(s - top)
+            e_new = jnp.exp(s_new - top)
+            inv = 1.0 / (jnp.sum(e, axis=-1, keepdims=True) + e_new)
+            p = (e * inv).astype(BF16)
+            p_new = (e_new * inv).astype(BF16).astype(F32)
+            outs = []
+            for n in range(KV_ROWS):
                 v2 = jnp.concatenate([vbuf[slot, n, 0], vbuf[slot, n, 1]], axis=1)
-                s = lax.dot_general(q2, k2, (((1,), (1,)), ((), ())), preferred_element_type=F32) * scale_qk
-                s = jnp.where(places < lens[b], s, -jnp.inf)
-                s_new = jnp.sum(q * kn[r, :], axis=-1, keepdims=True) * scale_qk
-                top = jnp.maximum(jnp.max(s, axis=-1, keepdims=True), s_new)
-                e = jnp.exp(s - top)
-                e_new = jnp.exp(s_new - top)
-                inv = 1.0 / (jnp.sum(e, axis=-1, keepdims=True) + e_new)
-                o = jnp.dot((e * inv).astype(BF16), v2, preferred_element_type=F32)
-                qs[r, :] = jnp.where(first_rows, o[:, :hd], o[:, hd:]) + (e_new * inv).astype(BF16).astype(F32) * vn[r, :]
+                o = jnp.dot(p[n * heads:(n + 1) * heads], v2, preferred_element_type=F32)
+                outs.append(jnp.where(first_rows, o[:, :hd], o[:, hd:]))
+            qs[r, :] = jnp.concatenate(outs, axis=0) + p_new * vn[r, :]
 
             @pl.when(i + KV_SLOTS < n_blocks)
             def _():
@@ -280,22 +302,37 @@
 
     def o_part(l, part):
         r = whole(part)
-
-        def step(j, c):
-            if part == DEC:
-                wo_copy(l, j).wait()
-            w = dbuf[j // o_per_slot, pl.ds(pl.multiple_of(lax.rem(j, o_per_slot) * o_depth, 16), o_depth), :]
-            sent(l, O, part, j)
-            pbuf[j, r, :] = jnp.dot(att[r, :], w, preferred_element_type=F32).astype(BF16)
-            p_copy(O, part, j).start()
-
-            @pl.when(j >= 1)
-            def _():
-                pair_sum(O, part, j - 1)
-            return c
-
-        lax.fori_loop(0, n_chunks, step, 0)
-        pair_sum(O, part, n_chunks - 1)
+        lag = 2
+
+        def step(i, c):
+            pair = (2 * i, 2 * i + 1)
+            for j in pair:
+                if part == DEC:
+                    wo_copy(l, j).wait()
+                sent(l, O, part, j)
+            prods = []
+            for j in pair:
+                w = dbuf[j // o_per_slot, pl.ds(pl.multiple_of(lax.rem(j, o_per_slot) * o_depth, 16), o_depth), :]
+                prods.append(jnp.dot(att[r, :], w, preferred_element_type=F32).astype(BF16))
+            for j, prod in zip(pair, prods):
+                pbuf[j, r, :] = prod
+                p_copy(O, part, j).start()
+
+            @pl.when(i >= lag)
+            def _():
+                for j in pair:
+                    pair_sum(O, part, j - 2 * lag)
+            return c
+
+        lax.fori_loop(0, n_chunks // 2, step, 0)
+        if l > 0 and part == DEC:
+            def pre_step(j, c):
+                finish(l - 1, M, PRE, j)
+                return c
+
+            lax.fori_loop(0, n_chunks, pre_step, 0)
+        for j in range(n_chunks - 2 * lag, n_chunks):
+            pair_sum(O, part, j)
 
     def gate_up(l):
         def block(j):
@@ -303,21 +340,17 @@
             h_wait(O, PRE, j)
             vals = h_o[j].astype(F32)
             add_squares(pl.ds(0, rows), vals)
-            a = (vals * pre[:, :1] * gain_m[l:l + 1, cols(j)]).astype(BF16)
-            slot = lax.rem(j, G_SLOTS)
-            wait(g_copies(l, j))
-
-            def mat(m, c):
+            a = (vals * pre[:, :1] * gain_m[l:l + 1, cols(j)].astype(F32)).astype(BF16)
+            for m in range(2):
+                g_copy(l, j, m).wait()
+                slot = lax.rem(2 * j + m, G_SLOTS)
                 for n in range(ff // CW):
-                    col = pl.ds(pl.multiple_of(m * ff + n * CW, CW), CW)
-                    acc[:, col] += jnp.dot(a, gbuf[slot, m, :, n * CW:(n + 1) * CW], preferred_element_type=F32)
-                return c
-
-            lax.fori_loop(0, 2, mat, 0)
-
-            @pl.when(j + G_SLOTS < n_chunks)
-            def _():
-                start(g_copies(l, j + G_SLOTS))
+                    acc[:, m * ff + n * CW:m * ff + (n + 1) * CW] += jnp.dot(a, gbuf[slot, :, n * CW:(n + 1) * CW], preferred_element_type=F32)
+                nxt = j + (G_SLOTS + m) // 2
+
+                @pl.when(nxt < n_chunks)
+                def _():
+                    g_copy(l, nxt, (G_SLOTS + m) % 2).start()
 
             @pl.when(j >= n_chunks - D_SLOTS)
             def _():
@@ -385,14 +418,24 @@
     barrier = pltpu.get_barrier_semaphore()
     for peer in (core_peer, x_peer):
         pl.semaphore_signal(barrier, inc=1, device_id=peer, device_id_type=MESH)
-    ssq[...] = jnp.zeros_like(ssq)
     for j in range(n_chunks):
         start(qkv_copies(0, j))
     for i in range(KV_SLOTS):
         start(kv_copies(0, i))
-    for j in range(n_chunks):
-        wo_copy(0, j).start()
     start(kv_pre_copies(0))
+    ssq[...] = jnp.zeros_like(ssq)
+
+    def place(b, c):
+        cos[pl.ds(b, 1), :] = jnp.full((1, hd), lens[b], jnp.int32).astype(F32)
+        return c
+
+    lax.fori_loop(0, dec, place, 0)
+    cos[pl.ds(dec, chunk), :] = (lax.broadcasted_iota(jnp.int32, (chunk, hd), 0) + lens[dec]).astype(F32)
+    angles = cos[...] * freq[...]
+    low = lax.broadcasted_iota(jnp.int32, (rows, hd), 1) < hd // 2
+    sines = jnp.sin(angles)
+    sin[...] = jnp.where(low, -sines, sines)
+    cos[...] = jnp.cos(angles)
     for j in range(n_chunks):
         x_load(j).wait()
 
@@ -410,8 +453,8 @@
         decode_attention(l)
         o_part(l, DEC)
         qkv_part(l, PRE)
-        for j in range(G_SLOTS):
-            start(g_copies(l, j))
+        for i in range(G_SLOTS):
+            g_copy(l, i // 2, i % 2).start()
         prefill_attention(l)
         o_part(l, PRE)
         acc[...] = jnp.zeros_like(acc)
@@ -444,7 +487,7 @@
             x_copy(M, part, j).wait_send()
 
 
-def step_call(lengths, x, cos_tab, sin_tab, attn_gain, mlp_gain, w_q, w_k, w_v, w_o, w_gate, w_up, w_down, k_cache, v_cache):
+def step_call(lengths, x, freq, attn_gain, mlp_gain, w_q, w_k, w_v, w_o, w_gate, w_up, w_down, k_cache, v_cache):
     rows, width = x.shape
     dec = lengths.shape[0] - 1
     chunk = rows - dec
@@ -461,10 +504,10 @@
     return pl.pallas_call(
         functools.partial(step_kernel, (dec, chunk)),
         out_shape=jax.ShapeDtypeStruct((rows, width), BF16),
-        in_specs=[smem, hbm, vmem, vmem, vmem, vmem] + [hbm] * 9,
+        in_specs=[smem, hbm, vmem, vmem, vmem] + [hbm] * 9,
         out_specs=hbm,
         scratch_shapes=[
-            buf((G_SLOTS, 2, CW, ff), BF16),
+            buf((G_SLOTS, CW, ff), BF16),
             buf((D_SLOTS, ff, CW), BF16),
             buf((rows, 2 * ff), F32),
             buf((rows, ff), BF16),
@@ -476,6 +519,8 @@
             buf((n_chunks, rows, CW), BF16),
             buf((rows, 128), F32),
             buf((rows, 128), F32),
+            buf((rows, hd), F32),
+            buf((rows, hd), F32),
             buf((KV_SLOTS, KV_ROWS, kv_heads, seq, hd), BF16),
             buf((KV_SLOTS, KV_ROWS, kv_heads, seq, hd), BF16),
             buf((kv_heads, seq, hd), BF16),
@@ -491,7 +536,7 @@
             sem((n_chunks,)),
             sem((n_chunks,)),
             sem((n_chunks,)),
-            sem((G_SLOTS, 2)),
+            sem((G_SLOTS,)),
             sem((D_SLOTS,)),
             sem((KV_SLOTS, 2)),
             sem((2,)),
@@ -505,7 +550,7 @@
         ],
         compiler_params=pltpu.CompilerParams(collective_id=0, has_side_effects=True, vmem_limit_bytes=67043328),
         name='decoder_step',
-    )(lengths, x, cos_tab, sin_tab, attn_gain, mlp_gain, w_q, w_k, w_v, w_o, w_gate, w_up, w_down, k_cache, v_cache)
+    )(lengths, x, freq, attn_gain, mlp_gain, w_q, w_k, w_v, w_o, w_gate, w_up, w_down, k_cache, v_cache)
 
 
 def solution(mesh):
@@ -515,15 +560,10 @@
     in_specs = (P('dp', None), P('dp'), P(), col_spec, col_spec, col_spec, row_spec, P(), col_spec, col_spec, row_spec, cache_spec, cache_spec)
 
     def body(x, lengths, attn_gain, w_q, w_k, w_v, w_o, mlp_gain, w_gate, w_up, w_down, k_cache, v_cache):
-        dec_rows = lengths.shape[0] - 1
-        chunk_len = x.shape[0] - dec_rows
         head_dim = k_cache.shape[-1]
-        positions = jnp.concatenate([lengths[:dec_rows], lengths[dec_rows] + jnp.arange(chunk_len, dtype=jnp.int32)])
-        freq_exps = jnp.arange(0, head_dim, 2, dtype=F32) / head_dim
-        angles = positions.astype(F32)[:, None] * jnp.power(ROPE_BASE, -freq_exps)[None, :]
-        cos_tab, sin_tab = jnp.cos(angles), jnp.sin(angles)
-        cos_tab = jnp.concatenate([cos_tab, cos_tab], axis=-1)
-        sin_tab = jnp.concatenate([-sin_tab, sin_tab], axis=-1)
-        return step_call(lengths, x, cos_tab, sin_tab, attn_gain.astype(F32), mlp_gain.astype(F32), w_q, w_k, w_v, w_o, w_gate, w_up, w_down, k_cache, v_cache)
+        exps = np.arange(0, head_dim, 2, dtype=np.float32) / np.float32(head_dim)
+        freq = np.power(np.float32(ROPE_BASE), -exps).astype(np.float32)
+        freq = jnp.asarray(np.concatenate([freq, freq])[None])
+        return step_call(lengths, x, freq, attn_gain, mlp_gain, w_q, w_k, w_v, w_o, w_gate, w_up, w_down, k_cache, v_cache)
 
     return jax.shard_map(body, mesh=mesh, in_specs=in_specs, out_specs=P('dp', None), check_vma=False)

time: 247 us -> 167 us (0.68)
  Pallas kernels: 237 us -> 163 us
  other arithmetic: 5.37 us -> 0 us
    pallas_call x1, Pallas kernels: 237 us -> 163 us  [step_call(): pl.pallas_call(functools.partial(step_kernel, (dec, chunk)), out_shape=ja...]
    convert_element_type x3 -> x0, other arithmetic: 3.43 us -> none  [the longest x1 1.36 us: body(): attn_gain.astype(F32)]
where the time goes in v3:
time: 167 us; the launch traced here: 166 us
  Pallas kernels  163 us (98%)
  local copies, waits for them, and re-layouts  3.18 us (2%)
    pallas_call x1, Pallas kernels, step_call(): pl.pallas_call(functools.partial(step_kernel, (dec, chunk)), out_shape=ja...  163 us

profile of v3, /device:TPU:0, one launch (start us, length us, event | category | flops | bytes accessed | tf_op | source)
XLA Modules:
  0.0 166.5 jit_solution(8213306708409011117)
XLA Ops:
  0.0 163.3 %decoder_step.1 = bf16[224,5120]{1,0:T(8,128)(2,1)} custom-call(s32[97]{0:T(128)} %lens.1, bf16[224,5120]{1,0:T(8,128)(2,1)} %x_in.1, f32[1,128]{1,0:T(1,128)} %constant.2.clone.freq, bf16[2,5120]{1,0:T(2,128)(2,1)} %gain_a.1, bf16[2,5120]{1,0:T(2,128)(2,1)} %gain_m.1, bf16[2,5120,1024]{2,1,0:T(8,128)(2,1)} %wq.1, bf16[2,5120,256]{2,1,0:T(8,128)(2,1)} %wk.1, ...), custom_call_target="tpu_custom_call" | custom-call | tf_op jit(solution)/shard_map/decoder_step/pallas_call | solution.py:504
  163.3 3.2 %copy.16 = bf16[224,5120]{1,0:T(8,128)(2,1)} copy(bf16[224,5120]{1,0:T(8,128)(2,1)} %decoder_step.1) | data formatting | bytes 4587520

commit v4 on v3

--- a/solution.py
+++ b/solution.py
@@ -16,8 +16,10 @@
 CW = 512
 G_SLOTS = 5
 D_SLOTS = 4
-KV_SLOTS = 2
-KV_ROWS = 16
+KV_SLOTS = 5
+KV_ROWS = 8
+ATT_SLOTS = 2
+GROUP = 5
 O, M = 0, 1
 DEC, PRE = 0, 1
 
@@ -181,26 +183,33 @@
     def qkv_part(l, part):
         r = whole(part)
         acc[r, :n_qkv] = jnp.zeros((size[part], n_qkv), F32)
-        n_pairs = n_chunks // 2
-
-        def pair_of(i):
-            return 2 * i, 2 * i + 1
+        n = GROUP if part == PRE else 2
+        steps = n_chunks // n
+        arriving = l > 0 and part == DEC
+
+        def chunks_of(i):
+            return tuple(n * i + t for t in range(n))
 
         def step(i, c):
-            if l > 0 and part == DEC:
-                for j in pair_of(i):
+            if arriving:
+                for j in chunks_of(i):
                     finish(l - 1, M, part, j)
 
                 @pl.when(i >= 1)
                 def _():
-                    qkv_block(l, part, pair_of(i - 1))
+                    qkv_block(l, part, chunks_of(i - 1))
             else:
-                qkv_block(l, part, pair_of(i))
-            return c
-
-        lax.fori_loop(0, n_pairs, step, 0)
-        if l > 0 and part == DEC:
-            qkv_block(l, part, pair_of(n_pairs - 1))
+                qkv_block(l, part, chunks_of(i))
+            if l == 0 and part == DEC:
+                @pl.when(i == 2)
+                def _():
+                    for j in range(n_chunks):
+                        wo_copy(l, j).start()
+            return c
+
+        lax.fori_loop(0, steps, step, 0)
+        if arriving:
+            qkv_block(l, part, chunks_of(steps - 1))
         scale = next_scale(r)
         c_tab, s_tab = cos[r, :], sin[r, :]
 
@@ -230,26 +239,25 @@
     def decode_attention(l):
         first_rows = lax.broadcasted_iota(jnp.int32, (heads, hd), 0) < group
         places = lax.broadcasted_iota(jnp.int32, (heads, seq), 1)
-        n_blocks = dec // KV_ROWS
+        n_slots = dec // KV_ROWS
+        step_rows = ATT_SLOTS * KV_ROWS
 
         def block(i, c):
-            wait(kv_copies(l, i))
-            slot = lax.rem(i, KV_SLOTS)
-            if l == 0:
-                @pl.when(i == n_blocks - KV_SLOTS)
-                def _():
-                    for j in range(n_chunks):
-                        wo_copy(l, j).start()
+            slots = []
+            for t in range(ATT_SLOTS):
+                wait(kv_copies(l, ATT_SLOTS * i + t))
+                slots.append(lax.rem(ATT_SLOTS * i + t, KV_SLOTS))
             scores = []
-            for n in range(KV_ROWS):
-                b = i * KV_ROWS + n
+            for n in range(step_rows):
+                b = i * step_rows + n
+                slot, m = slots[n // KV_ROWS], n % KV_ROWS
                 q = qs[pl.ds(pl.multiple_of(b * heads, heads), heads), :]
                 zero = jnp.zeros_like(q)
                 q2 = jnp.concatenate([jnp.where(first_rows, q, zero), jnp.where(first_rows, zero, q)], axis=1).astype(BF16)
-                k2 = jnp.concatenate([kbuf[slot, n, 0], kbuf[slot, n, 1]], axis=1)
+                k2 = jnp.concatenate([kbuf[slot, m, 0], kbuf[slot, m, 1]], axis=1)
                 s = lax.dot_general(q2, k2, (((1,), (1,)), ((), ())), preferred_element_type=F32) * scale_qk
                 scores.append(jnp.where(places < lens[b], s, -jnp.inf))
-            r = pl.ds(pl.multiple_of(i * KV_ROWS * heads, KV_ROWS * heads), KV_ROWS * heads)
+            r = pl.ds(pl.multiple_of(i * step_rows * heads, step_rows * heads), step_rows * heads)
             s = jnp.concatenate(scores, axis=0)
             s_new = jnp.sum(qs[r, :] * kn[r, :], axis=-1, keepdims=True) * scale_qk
             top = jnp.maximum(jnp.max(s, axis=-1, keepdims=True), s_new)
@@ -259,114 +267,134 @@
             p = (e * inv).astype(BF16)
             p_new = (e_new * inv).astype(BF16).astype(F32)
             outs = []
-            for n in range(KV_ROWS):
-                v2 = jnp.concatenate([vbuf[slot, n, 0], vbuf[slot, n, 1]], axis=1)
+            for n in range(step_rows):
+                slot, m = slots[n // KV_ROWS], n % KV_ROWS
+                v2 = jnp.concatenate([vbuf[slot, m, 0], vbuf[slot, m, 1]], axis=1)
                 o = jnp.dot(p[n * heads:(n + 1) * heads], v2, preferred_element_type=F32)
                 outs.append(jnp.where(first_rows, o[:, :hd], o[:, hd:]))
             qs[r, :] = jnp.concatenate(outs, axis=0) + p_new * vn[r, :]
 
-            @pl.when(i + KV_SLOTS < n_blocks)
-            def _():
-                start(kv_copies(l, i + KV_SLOTS))
-            return c
-
-        lax.fori_loop(0, n_blocks, block, 0)
+            for t in range(ATT_SLOTS):
+                nxt = ATT_SLOTS * i + t + KV_SLOTS
+
+                @pl.when(nxt < n_slots)
+                def _():
+                    start(kv_copies(l, nxt))
+            return c
+
+        lax.fori_loop(0, n_slots // ATT_SLOTS, block, 0)
         for h in range(heads):
             att[:dec, h * hd:(h + 1) * hd] = qs[pl.ds(h, dec, stride=heads), :].astype(BF16)
 
     def prefill_attention(l):
         wait(kv_pre_copies(l))
-        n_old = lens[dec]
-        old = lax.broadcasted_iota(jnp.int32, (chunk, seq), 1) < n_old
-        causal = lax.broadcasted_iota(jnp.int32, (chunk, chunk), 1) <= lax.broadcasted_iota(jnp.int32, (chunk, chunk), 0)
-
-        def heads_step(i, c):
-            for g in range(kv_heads):
-                col = pl.ds(pl.multiple_of((g * group + i) * hd, hd), hd)
-                q = qp[:, col]
-                kv_col = slice(g * hd, (g + 1) * hd)
-                s = lax.dot_general(q, kpre[g], (((1,), (1,)), ((), ())), preferred_element_type=F32) * scale_qk
-                s = jnp.where(old, s, -jnp.inf)
-                t = lax.dot_general(q, kp[:, kv_col], (((1,), (1,)), ((), ())), preferred_element_type=F32) * scale_qk
-                t = jnp.where(causal, t, -jnp.inf)
-                top = jnp.maximum(jnp.max(s, axis=-1, keepdims=True), jnp.max(t, axis=-1, keepdims=True))
-                es = jnp.exp(s - top)
-                et = jnp.exp(t - top)
-                inv = 1.0 / (jnp.sum(es, axis=-1, keepdims=True) + jnp.sum(et, axis=-1, keepdims=True))
-                o = jnp.dot((es * inv).astype(BF16), vpre[g], preferred_element_type=F32)
-                o += jnp.dot((et * inv).astype(BF16), vp[:, kv_col], preferred_element_type=F32)
-                att[pl.ds(dec, chunk), col] = o.astype(BF16)
-            return c
-
-        lax.fori_loop(0, group, heads_step, 0)
+        old = jnp.where(lax.broadcasted_iota(jnp.int32, (1, seq), 1) < lens[dec], 0.0, -jnp.inf)
+        causal = jnp.where(lax.broadcasted_iota(jnp.int32, (chunk, chunk), 1) <= lax.broadcasted_iota(jnp.int32, (chunk, chunk), 0), 0.0, -jnp.inf)
+        causal = jnp.concatenate([causal] * group, axis=0)
+        for g in range(kv_heads):
+            q = jnp.concatenate([qp[:, (g * group + i) * hd:(g * group + i + 1) * hd] for i in range(group)], axis=0)
+            kv_col = slice(g * hd, (g + 1) * hd)
+            s = lax.dot_general(q, kpre[g], (((1,), (1,)), ((), ())), preferred_element_type=F32) * scale_qk + old
+            t = lax.dot_general(q, kp[:, kv_col], (((1,), (1,)), ((), ())), preferred_element_type=F32) * scale_qk + causal
+            top = jnp.maximum(jnp.max(s, axis=-1, keepdims=True), jnp.max(t, axis=-1, keepdims=True))
+            es = jnp.exp(s - top)
+            et = jnp.exp(t - top)
+            inv = 1.0 / (jnp.sum(es, axis=-1, keepdims=True) + jnp.sum(et, axis=-1, keepdims=True))
+            o = jnp.dot((es * inv).astype(BF16), vpre[g], preferred_element_type=F32)
+            o += jnp.dot((et * inv).astype(BF16), vp[:, kv_col], preferred_element_type=F32)
+            for i in range(group):
+                att[dec:, (g * group + i) * hd:(g * group + i + 1) * hd] = o[i * chunk:(i + 1) * chunk].astype(BF16)
 
     def o_part(l, part):
         r = whole(part)
-        lag = 2
 
         def step(i, c):
-            pair = (2 * i, 2 * i + 1)
-            for j in pair:
+            these = tuple(GROUP * i + t for t in range(GROUP))
+            for j in these:
                 if part == DEC:
                     wo_copy(l, j).wait()
                 sent(l, O, part, j)
-            prods = []
-            for j in pair:
+            for j in these:
                 w = dbuf[j // o_per_slot, pl.ds(pl.multiple_of(lax.rem(j, o_per_slot) * o_depth, 16), o_depth), :]
-                prods.append(jnp.dot(att[r, :], w, preferred_element_type=F32).astype(BF16))
-            for j, prod in zip(pair, prods):
-                pbuf[j, r, :] = prod
+                pbuf[j, r, :] = jnp.dot(att[r, :], w, preferred_element_type=F32).astype(BF16)
                 p_copy(O, part, j).start()
 
-            @pl.when(i >= lag)
+            @pl.when(i >= 1)
             def _():
-                for j in pair:
-                    pair_sum(O, part, j - 2 * lag)
-            return c
-
-        lax.fori_loop(0, n_chunks // 2, step, 0)
-        if l > 0 and part == DEC:
-            def pre_step(j, c):
-                finish(l - 1, M, PRE, j)
-                return c
-
-            lax.fori_loop(0, n_chunks, pre_step, 0)
-        for j in range(n_chunks - 2 * lag, n_chunks):
-            pair_sum(O, part, j)
-
-    def gate_up(l):
+                for j in these:
+                    pair_sum(O, part, j - GROUP)
+            return c
+
+        lax.fori_loop(0, n_chunks // GROUP, step, 0)
+
+        def rest():
+            for j in range(n_chunks - GROUP, n_chunks):
+                pair_sum(O, part, j)
+
+        return rest
+
+    def gate_up(l, rest):
+        def operand(r, j):
+            vals = h_o[j, r, :].astype(F32)
+            add_squares(r, vals)
+            return (vals * pre[r, :1] * gain_m[l:l + 1, cols(j)].astype(F32)).astype(BF16)
+
+        def release(j, m):
+            nxt = j + (G_SLOTS + m) // 2
+
+            @pl.when(nxt < n_chunks)
+            def _():
+                g_copy(l, nxt, (G_SLOTS + m) % 2).start()
+
+        def first_block(part):
+            r = whole(part)
+            a = operand(r, 0)
+            for m in range(2):
+                if part == DEC:
+                    g_copy(l, 0, m).wait()
+                for n in range(ff // CW):
+                    acc[r, m * ff + n * CW:m * ff + (n + 1) * CW] = jnp.dot(a, gbuf[m, :, n * CW:(n + 1) * CW], preferred_element_type=F32)
+                if part == PRE:
+                    g_copy(l, (G_SLOTS + m) // 2, (G_SLOTS + m) % 2).start()
+
         def block(j):
             h_wait(O, DEC, j)
             h_wait(O, PRE, j)
-            vals = h_o[j].astype(F32)
-            add_squares(pl.ds(0, rows), vals)
-            a = (vals * pre[:, :1] * gain_m[l:l + 1, cols(j)].astype(F32)).astype(BF16)
+            a = operand(pl.ds(0, rows), j)
             for m in range(2):
                 g_copy(l, j, m).wait()
                 slot = lax.rem(2 * j + m, G_SLOTS)
                 for n in range(ff // CW):
                     acc[:, m * ff + n * CW:m * ff + (n + 1) * CW] += jnp.dot(a, gbuf[slot, :, n * CW:(n + 1) * CW], preferred_element_type=F32)
-                nxt = j + (G_SLOTS + m) // 2
-
-                @pl.when(nxt < n_chunks)
-                def _():
-                    g_copy(l, nxt, (G_SLOTS + m) % 2).start()
+                release(j, m)
 
             @pl.when(j >= n_chunks - D_SLOTS)
             def _():
                 d_copy(l, j - (n_chunks - D_SLOTS)).start()
 
+        def dec_step(j, c):
+            finish(l, O, DEC, j)
+            return c
+
+        lax.fori_loop(0, GROUP, dec_step, 0)
+        rest()
+        lax.fori_loop(GROUP, n_chunks, dec_step, 0)
+        finish(l, O, PRE, 0)
+        h_wait(O, DEC, 0)
+        first_block(DEC)
+        finish(l, O, PRE, 1)
+        h_wait(O, PRE, 0)
+        first_block(PRE)
+
         def step(j, c):
-            finish(l, O, DEC, j)
-            finish(l, O, PRE, j)
-
-            @pl.when(j >= 1)
+            @pl.when(j + 1 < n_chunks)
             def _():
-                block(j - 1)
-            return c
-
-        lax.fori_loop(0, n_chunks, step, 0)
-        block(n_chunks - 1)
+                finish(l, O, PRE, j + 1)
+
+            block(j)
+            return c
+
+        lax.fori_loop(1, n_chunks, step, 0)
         scale = next_scale(pl.ds(0, rows))
 
         def act_step(n, c):
@@ -391,7 +419,10 @@
                 d_copy(l, j + D_SLOTS).start()
 
             if l + 1 < layers:
-                start(qkv_copies(l + 1, j))
+                @pl.when(j == n_chunks - D_SLOTS - 1)
+                def _():
+                    for n in range(n_chunks):
+                        start(qkv_copies(l + 1, n))
 
             @pl.when(j >= 1)
             def _():
@@ -451,40 +482,72 @@
     for l in range(layers):
         qkv_part(l, DEC)
         decode_attention(l)
-        o_part(l, DEC)
+        rest = o_part(l, DEC)
+        if l > 0:
+            def pre_step(j, c):
+                finish(l - 1, M, PRE, j)
+                return c
+
+            lax.fori_loop(0, n_chunks, pre_step, 0)
+            rest()
         qkv_part(l, PRE)
+        if l == 0:
+            rest()
         for i in range(G_SLOTS):
             g_copy(l, i // 2, i % 2).start()
         prefill_attention(l)
-        o_part(l, PRE)
-        acc[...] = jnp.zeros_like(acc)
-        gate_up(l)
+        gate_up(l, o_part(l, PRE))
         down(l)
 
     def out_copy(part, j):
         r = whole(part)
         return pltpu.make_async_copy(h_m.at[j, r, :], y.at[r, cols(j)], y_sem.at[part, j])
 
-    for part in (DEC, PRE):
-        def out_step(j, c):
-            finish(layers - 1, M, part, j)
-
-            @pl.when(j >= 1)
-            def _():
-                h_wait(M, part, j - 1)
-                out_copy(part, j - 1).start()
-            return c
-
-        lax.fori_loop(0, n_chunks, out_step, 0)
-        h_wait(M, part, n_chunks - 1)
-        out_copy(part, n_chunks - 1).start()
-    for part in (DEC, PRE):
-        for j in range(n_chunks):
-            out_copy(part, j).wait()
-            h_copy(O, part, j).wait_send()
-            h_copy(M, part, j).wait_send()
-            p_copy(M, part, j).wait_send()
-            x_copy(M, part, j).wait_send()
+    def out_dec(j, c):
+        finish(layers - 1, M, DEC, j)
+
+        @pl.when(j >= 1)
+        def _():
+            h_wait(M, DEC, j - 1)
+            out_copy(DEC, j - 1).start()
+
+        h_copy(O, DEC, j).wait_send()
+        h_copy(O, PRE, j).wait_send()
+        p_copy(M, DEC, j).wait_send()
+        p_copy(M, PRE, j).wait_send()
+        return c
+
+    lax.fori_loop(0, n_chunks, out_dec, 0)
+    h_wait(M, DEC, n_chunks - 1)
+    out_copy(DEC, n_chunks - 1).start()
+
+    def out_pre(j, c):
+        finish(layers - 1, M, PRE, j)
+        x_copy(M, DEC, j).wait_send()
+        h_copy(M, DEC, j).wait_send()
+
+        @pl.when(j >= 1)
+        def _():
+            h_wait(M, PRE, j - 1)
+            out_copy(PRE, j - 1).start()
+            out_copy(DEC, j - 1).wait()
+            x_copy(M, PRE, j - 1).wait_send()
+
+        @pl.when(j >= 2)
+        def _():
+            h_copy(M, PRE, j - 2).wait_send()
+            out_copy(PRE, j - 2).wait()
+        return c
+
+    lax.fori_loop(0, n_chunks, out_pre, 0)
+    last = n_chunks - 1
+    h_wait(M, PRE, last)
+    out_copy(PRE, last).start()
+    x_copy(M, PRE, last).wait_send()
+    out_copy(DEC, last).wait()
+    for j in (last - 1, last):
+        h_copy(M, PRE, j).wait_send()
+        out_copy(PRE, j).wait()
 
 
 def step_call(lengths, x, freq, attn_gain, mlp_gain, w_q, w_k, w_v, w_o, w_gate, w_up, w_down, k_cache, v_cache):

time: 167 us -> 168 us (level)
  Pallas kernels: 163 us -> 165 us
where the time goes in v4:
time: 168 us
  Pallas kernels  165 us (98%)
  local copies, waits for them, and re-layouts  3.18 us (2%)
    pallas_call x1, Pallas kernels, step_call(): pl.pallas_call(functools.partial(step_kernel, (dec, chunk)), out_shape=ja...  165 us

profile of v4, /device:TPU:0, one launch (start us, length us, event | category | flops | bytes accessed | tf_op | source)
XLA Modules:
  0.0 168.1 jit_solution(15010039741389226695)
XLA Ops:
  0.0 164.9 %decoder_step.1 = bf16[224,5120]{1,0:T(8,128)(2,1)} custom-call(s32[97]{0:T(128)} %lens.1, bf16[224,5120]{1,0:T(8,128)(2,1)} %x_in.1, f32[1,128]{1,0:T(1,128)} %constant.2.clone.freq, bf16[2,5120]{1,0:T(2,128)(2,1)} %gain_a.1, bf16[2,5120]{1,0:T(2,128)(2,1)} %gain_m.1, bf16[2,5120,1024]{2,1,0:T(8,128)(2,1)} %wq.1, bf16[2,5120,256]{2,1,0:T(8,128)(2,1)} %wk.1, ...), custom_call_target="tpu_custom_call" | custom-call | tf_op jit(solution)/shard_map/decoder_step/pallas_call | solution.py:567
  164.9 3.2 %copy.16 = bf16[224,5120]{1,0:T(8,128)(2,1)} copy(bf16[224,5120]{1,0:T(8,128)(2,1)} %decoder_step.1) | data formatting | bytes 4587520

commit v5 on v4

--- a/solution.py
+++ b/solution.py
@@ -19,6 +19,7 @@
 KV_SLOTS = 5
 KV_ROWS = 8
 ATT_SLOTS = 2
+AHEAD = 7
 GROUP = 5
 O, M = 0, 1
 DEC, PRE = 0, 1
@@ -27,7 +28,7 @@
 def step_kernel(dims, lens, x_in, freq, gain_a, gain_m, wq, wk, wv, wo, wg, wu, wd, kc, vc, y,
                 gbuf, dbuf, acc, act, pbuf, rbuf, xb_o, xb_m, h_o, h_m, ssq, pre, cos, sin, kbuf, vbuf, kpre, vpre,
                 qs, kn, vn, qp, kp, vp, att,
-                q_sem, w_sem, k_sem, v_sem, g_sem, d_sem, kv_sem, kvp_sem, y_sem, p_ss, p_rs, x_ss, x_rs, h_ss, h_rs):
+                q_sem, w_sem, g_sem, d_sem, kv_sem, io_sem, p_ss, p_rs, x_ss, x_rs, h_ss, h_rs):
     dec, chunk = dims
     rows = dec + chunk
     width = x_in.shape[1]
@@ -71,7 +72,7 @@
     hs = (h_o, h_m)
 
     def x_load(j):
-        return pltpu.make_async_copy(x_in.at[:, cols(j)], h_m.at[j], y_sem.at[0, j])
+        return pltpu.make_async_copy(x_in.at[:, cols(j)], h_m.at[j], io_sem.at[0])
 
     def wo_copy(l, j):
         return pltpu.make_async_copy(wo.at[l, :, cols(j)], dbuf.at[j // o_per_slot, pl.ds(pl.multiple_of(lax.rem(j, o_per_slot) * o_depth, 16), o_depth), :], w_sem.at[j])
@@ -95,8 +96,13 @@
             return dst.at[:, pl.ds(pl.multiple_of(left + off, 128), n)]
 
         return (pltpu.make_async_copy(wq.at[l, cols(j), :], at(0, q_cols), q_sem.at[j]),
-                pltpu.make_async_copy(wk.at[l, cols(j), :], at(q_cols, k_cols), k_sem.at[j]),
-                pltpu.make_async_copy(wv.at[l, cols(j), :], at(q_cols + k_cols, k_cols), v_sem.at[j]))
+                pltpu.make_async_copy(wk.at[l, cols(j), :], at(q_cols, k_cols), q_sem.at[j]),
+                pltpu.make_async_copy(wv.at[l, cols(j), :], at(q_cols + k_cols, k_cols), q_sem.at[j]))
+
+    def qkv_wait(j):
+        slot, left = qkv_place(j)
+        dst = gbuf.at[slot, :, pl.ds(pl.multiple_of(left, 128), n_qkv)]
+        pltpu.make_async_copy(dst, dst, q_sem.at[j]).wait()
 
     def kv_copies(l, i):
         slot = lax.rem(i, KV_SLOTS)
@@ -105,8 +111,8 @@
                 pltpu.make_async_copy(vc.at[l, src], vbuf.at[slot], kv_sem.at[slot, 1]))
 
     def kv_pre_copies(l):
-        return (pltpu.make_async_copy(kc.at[l, dec], kpre, kvp_sem.at[0]),
-                pltpu.make_async_copy(vc.at[l, dec], vpre, kvp_sem.at[1]))
+        return (pltpu.make_async_copy(kc.at[l, dec], kpre, io_sem.at[1]),
+                pltpu.make_async_copy(vc.at[l, dec], vpre, io_sem.at[2]))
 
     def start(copies):
         for c in copies:
@@ -117,16 +123,16 @@
             c.wait()
 
     def p_copy(ar, part, j):
-        return pltpu.make_async_remote_copy(pbuf.at[j, oth(part), :], rbuf.at[j, landed(part), :], p_ss.at[ar, part, j], p_rs.at[ar, part, j], device_id=core_peer, device_id_type=MESH)
+        return pltpu.make_async_remote_copy(pbuf.at[j, oth(part), :], rbuf.at[j, landed(part), :], p_ss.at[part, j], p_rs.at[part, j], device_id=core_peer, device_id_type=MESH)
 
     def x_copy(ar, part, j):
-        return pltpu.make_async_remote_copy(pbuf.at[j, own(part), :], xbs[ar].at[j, landed(part), :], x_ss.at[ar, part, j], x_rs.at[ar, part, j], device_id=x_peer, device_id_type=MESH)
+        return pltpu.make_async_remote_copy(pbuf.at[j, own(part), :], xbs[ar].at[j, landed(part), :], x_ss.at[part, j], x_rs.at[ar, part, j], device_id=x_peer, device_id_type=MESH)
 
     def h_copy(ar, part, j):
-        return pltpu.make_async_remote_copy(hs[ar].at[j, own(part), :], hs[ar].at[j, own(part), :], h_ss.at[ar, part, j], h_rs.at[ar, part, j], device_id=core_peer, device_id_type=MESH)
+        return pltpu.make_async_remote_copy(hs[ar].at[j, own(part), :], hs[ar].at[j, own(part), :], h_ss.at[part, j], h_rs.at[part, j], device_id=core_peer, device_id_type=MESH)
 
     def h_wait(ar, part, j):
-        pltpu.make_async_remote_copy(hs[ar].at[j, oth(part), :], hs[ar].at[j, oth(part), :], h_ss.at[ar, part, j], h_rs.at[ar, part, j], device_id=core_peer, device_id_type=MESH).wait_recv()
+        pltpu.make_async_remote_copy(hs[ar].at[j, oth(part), :], hs[ar].at[j, oth(part), :], h_ss.at[part, j], h_rs.at[part, j], device_id=core_peer, device_id_type=MESH).wait_recv()
 
     def sent(l, ar, part, j):
         if l > 0 or ar == M:
@@ -142,8 +148,8 @@
         x_copy(ar, part, j).wait_recv()
         total = pbuf[j, own(part), :].astype(F32) + xbs[ar][j, landed(part), :].astype(F32)
         resid = hs[1 - ar][j, own(part), :].astype(F32)
-        if l > 0:
-            h_copy(ar, part, j).wait_send()
+        if l > 0 or ar == M:
+            h_copy(1 - ar, part, j).wait_send()
         hs[ar][j, own(part), :] = (resid + total).astype(BF16)
         h_copy(ar, part, j).start()
 
@@ -172,7 +178,7 @@
             add_squares(r, vals)
             a.append((vals * pre[r, :1] * gain_a[l:l + 1, cols(j)].astype(F32)).astype(BF16))
             if part == DEC:
-                wait(qkv_copies(l, j))
+                qkv_wait(j)
         for n in range(n_qkv // CW):
             total = acc[r, n * CW:(n + 1) * CW]
             for j, a_j in zip(pair, a):
@@ -200,11 +206,6 @@
                     qkv_block(l, part, chunks_of(i - 1))
             else:
                 qkv_block(l, part, chunks_of(i))
-            if l == 0 and part == DEC:
-                @pl.when(i == 2)
-                def _():
-                    for j in range(n_chunks):
-                        wo_copy(l, j).start()
             return c
 
         lax.fori_loop(0, steps, step, 0)
@@ -247,6 +248,11 @@
             for t in range(ATT_SLOTS):
                 wait(kv_copies(l, ATT_SLOTS * i + t))
                 slots.append(lax.rem(ATT_SLOTS * i + t, KV_SLOTS))
+            if l == 0:
+                @pl.when(i == 2)
+                def _():
+                    for j in range(n_chunks):
+                        wo_copy(l, j).start()
             scores = []
             for n in range(step_rows):
                 b = i * step_rows + n
@@ -317,6 +323,7 @@
             for j in these:
                 w = dbuf[j // o_per_slot, pl.ds(pl.multiple_of(lax.rem(j, o_per_slot) * o_depth, 16), o_depth), :]
                 pbuf[j, r, :] = jnp.dot(att[r, :], w, preferred_element_type=F32).astype(BF16)
+            for j in these:
                 p_copy(O, part, j).start()
 
             @pl.when(i >= 1)
@@ -327,13 +334,7 @@
 
         lax.fori_loop(0, n_chunks // GROUP, step, 0)
 
-        def rest():
-            for j in range(n_chunks - GROUP, n_chunks):
-                pair_sum(O, part, j)
-
-        return rest
-
-    def gate_up(l, rest):
+    def gate_up(l):
         def operand(r, j):
             vals = h_o[j, r, :].astype(F32)
             add_squares(r, vals)
@@ -377,8 +378,11 @@
             return c
 
         lax.fori_loop(0, GROUP, dec_step, 0)
-        rest()
-        lax.fori_loop(GROUP, n_chunks, dec_step, 0)
+        for j in range(GROUP, n_chunks):
+            if j >= AHEAD:
+                pair_sum(O, DEC, j)
+            pair_sum(O, PRE, j)
+        lax.fori_loop(GROUP, AHEAD, dec_step, 0)
         finish(l, O, PRE, 0)
         h_wait(O, DEC, 0)
         first_block(DEC)
@@ -389,6 +393,10 @@
         def step(j, c):
             @pl.when(j + 1 < n_chunks)
             def _():
+                @pl.when(j + 1 >= AHEAD)
+                def _():
+                    finish(l, O, DEC, j + 1)
+
                 finish(l, O, PRE, j + 1)
 
             block(j)
@@ -419,10 +427,12 @@
                 d_copy(l, j + D_SLOTS).start()
 
             if l + 1 < layers:
-                @pl.when(j == n_chunks - D_SLOTS - 1)
-                def _():
-                    for n in range(n_chunks):
-                        start(qkv_copies(l + 1, n))
+                for n in range(3):
+                    nxt = 3 * (j - (n_chunks - D_SLOTS)) + n
+
+                    @pl.when((nxt >= 0) & (nxt < n_chunks))
+                    def _():
+                        start(qkv_copies(l + 1, nxt))
 
             @pl.when(j >= 1)
             def _():
@@ -467,8 +477,7 @@
     sines = jnp.sin(angles)
     sin[...] = jnp.where(low, -sines, sines)
     cos[...] = jnp.cos(angles)
-    for j in range(n_chunks):
-        x_load(j).wait()
+    pltpu.make_async_copy(h_m, h_m, io_sem.at[0]).wait()
 
     def sq_step(j, c):
         add_squares(pl.ds(0, rows), h_m[j].astype(F32))
@@ -482,26 +491,29 @@
     for l in range(layers):
         qkv_part(l, DEC)
         decode_attention(l)
-        rest = o_part(l, DEC)
+        o_part(l, DEC)
         if l > 0:
             def pre_step(j, c):
                 finish(l - 1, M, PRE, j)
                 return c
 
             lax.fori_loop(0, n_chunks, pre_step, 0)
-            rest()
+            for j in range(GROUP, AHEAD):
+                pair_sum(O, DEC, j)
         qkv_part(l, PRE)
         if l == 0:
-            rest()
+            for j in range(GROUP, AHEAD):
+                pair_sum(O, DEC, j)
         for i in range(G_SLOTS):
             g_copy(l, i // 2, i % 2).start()
         prefill_attention(l)
-        gate_up(l, o_part(l, PRE))
+        o_part(l, PRE)
+        gate_up(l)
         down(l)
 
     def out_copy(part, j):
         r = whole(part)
-        return pltpu.make_async_copy(h_m.at[j, r, :], y.at[r, cols(j)], y_sem.at[part, j])
+        return pltpu.make_async_copy(h_m.at[j, r, :], y.at[r, cols(j)], io_sem.at[3 + part])
 
     def out_dec(j, c):
         finish(layers - 1, M, DEC, j)
@@ -511,8 +523,6 @@
             h_wait(M, DEC, j - 1)
             out_copy(DEC, j - 1).start()
 
-        h_copy(O, DEC, j).wait_send()
-        h_copy(O, PRE, j).wait_send()
         p_copy(M, DEC, j).wait_send()
         p_copy(M, PRE, j).wait_send()
         return c
@@ -530,13 +540,11 @@
         def _():
             h_wait(M, PRE, j - 1)
             out_copy(PRE, j - 1).start()
-            out_copy(DEC, j - 1).wait()
             x_copy(M, PRE, j - 1).wait_send()
 
         @pl.when(j >= 2)
         def _():
             h_copy(M, PRE, j - 2).wait_send()
-            out_copy(PRE, j - 2).wait()
         return c
 
     lax.fori_loop(0, n_chunks, out_pre, 0)
@@ -544,10 +552,11 @@
     h_wait(M, PRE, last)
     out_copy(PRE, last).start()
     x_copy(M, PRE, last).wait_send()
-    out_copy(DEC, last).wait()
     for j in (last - 1, last):
         h_copy(M, PRE, j).wait_send()
-        out_copy(PRE, j).wait()
+    for part in (DEC, PRE):
+        done = h_m.at[:, whole(part), :]
+        pltpu.make_async_copy(done, done, io_sem.at[3 + part]).wait()
 
 
 def step_call(lengths, x, freq, attn_gain, mlp_gain, w_q, w_k, w_v, w_o, w_gate, w_up, w_down, k_cache, v_cache):
@@ -597,19 +606,16 @@
             buf((rows, q_cols), BF16),
             sem((n_chunks,)),
             sem((n_chunks,)),
-            sem((n_chunks,)),
-            sem((n_chunks,)),
             sem((G_SLOTS,)),
             sem((D_SLOTS,)),
             sem((KV_SLOTS, 2)),
-            sem((2,)),
+            sem((5,)),
+            sem((2, n_chunks)),
+            sem((2, n_chunks)),
             sem((2, n_chunks)),
             sem((2, 2, n_chunks)),
-            sem((2, 2, n_chunks)),
-            sem((2, 2, n_chunks)),
-            sem((2, 2, n_chunks)),
-            sem((2, 2, n_chunks)),
-            sem((2, 2, n_chunks)),
+            sem((2, n_chunks)),
+            sem((2, n_chunks)),
         ],
         compiler_params=pltpu.CompilerParams(collective_id=0, has_side_effects=True, vmem_limit_bytes=67043328),
         name='decoder_step',

time: 168 us -> 158 us (0.940)
  Pallas kernels: 165 us -> 155 us
    pallas_call x1, Pallas kernels: 165 us -> 155 us  [step_call(): pl.pallas_call(functools.partial(step_kernel, (dec, chunk)), out_shape=ja...]
where the time goes in v5:
time: 158 us
  Pallas kernels  155 us (98%)
  local copies, waits for them, and re-layouts  3.18 us (2%)
    pallas_call x1, Pallas kernels, step_call(): pl.pallas_call(functools.partial(step_kernel, (dec, chunk)), out_shape=ja...  155 us
    unnamed x1, local copies, waits for them, and re-layouts  3.18 us

profile of v5, /device:TPU:0, one launch (start us, length us, event | category | flops | bytes accessed | tf_op | source)
XLA Modules:
  0.0 157.9 jit_solution(6957802988892708058)
XLA Ops:
  0.0 154.7 %decoder_step.1 = bf16[224,5120]{1,0:T(8,128)(2,1)} custom-call(s32[97]{0:T(128)} %lens.1, bf16[224,5120]{1,0:T(8,128)(2,1)} %x_in.1, f32[1,128]{1,0:T(1,128)} %constant.2.clone.freq, bf16[2,5120]{1,0:T(2,128)(2,1)} %gain_a.1, bf16[2,5120]{1,0:T(2,128)(2,1)} %gain_m.1, bf16[2,5120,1024]{2,1,0:T(8,128)(2,1)} %wq.1, bf16[2,5120,256]{2,1,0:T(8,128)(2,1)} %wk.1, ...), custom_call_target="tpu_custom_call" | custom-call | tf_op jit(solution)/shard_map/decoder_step/pallas_call | solution.py:576
  154.7 3.2 %copy.16 = bf16[224,5120]{1,0:T(8,128)(2,1)} copy(bf16[224,5120]{1,0:T(8,128)(2,1)} %decoder_step.1) | data formatting | bytes 4587520

commit v6 on v5

--- a/solution.py
+++ b/solution.py
@@ -20,14 +20,15 @@
 KV_ROWS = 8
 ATT_SLOTS = 2
 AHEAD = 7
+STACK = 4
 GROUP = 5
 O, M = 0, 1
 DEC, PRE = 0, 1
 
 
 def step_kernel(dims, lens, x_in, freq, gain_a, gain_m, wq, wk, wv, wo, wg, wu, wd, kc, vc, y,
-                gbuf, dbuf, acc, act, pbuf, rbuf, xb_o, xb_m, h_o, h_m, ssq, pre, cos, sin, kbuf, vbuf, kpre, vpre,
-                qs, kn, vn, qp, kp, vp, att,
+                gbuf, dbuf, abuf, acc, act, pbuf, rbuf, xb_o, xb_m, h_o, h_m, ssq, pre, cos, sin, kbuf, vbuf, kpre, vpre,
+                qs, kn, vn,
                 q_sem, w_sem, g_sem, d_sem, kv_sem, io_sem, p_ss, p_rs, x_ss, x_rs, h_ss, h_rs):
     dec, chunk = dims
     rows = dec + chunk
@@ -68,6 +69,10 @@
     def cols(j):
         return pl.ds(pl.multiple_of(j * CW, CW), CW)
 
+    att = act.at[:, pl.ds(0, q_cols)]
+    kp = act.at[pl.ds(0, chunk), pl.ds(q_cols, k_cols)]
+    vp = act.at[pl.ds(0, chunk), pl.ds(q_cols + k_cols, k_cols)]
+
     xbs = (xb_o, xb_m)
     hs = (h_o, h_m)
 
@@ -86,7 +91,7 @@
         return pltpu.make_async_copy(wd.at[l, :, cols(j)], dbuf.at[slot], d_sem.at[slot])
 
     def qkv_place(j):
-        return j // 2, lax.rem(j, 2) * (ff // 2)
+        return j // 2, (j % 2) * (ff // 2)
 
     def qkv_copies(l, j):
         slot, left = qkv_place(j)
@@ -186,31 +191,40 @@
                 total += jnp.dot(a_j, gbuf[slot, :, pl.ds(pl.multiple_of(left + n * CW, 128), CW)], preferred_element_type=F32)
             acc[r, n * CW:(n + 1) * CW] = total
 
-    def qkv_part(l, part):
-        r = whole(part)
-        acc[r, :n_qkv] = jnp.zeros((size[part], n_qkv), F32)
-        n = GROUP if part == PRE else 2
-        steps = n_chunks // n
-        arriving = l > 0 and part == DEC
-
-        def chunks_of(i):
-            return tuple(n * i + t for t in range(n))
+    def qkv_begin(part):
+        acc[whole(part), :n_qkv] = jnp.zeros((size[part], n_qkv), F32)
+
+    def qkv_decode(l):
+        qkv_begin(DEC)
+        steps = n_chunks // 2
+
+        def pair(i):
+            return 2 * i, 2 * i + 1
 
         def step(i, c):
-            if arriving:
-                for j in chunks_of(i):
-                    finish(l - 1, M, part, j)
+            if l > 0:
+                for j in pair(i):
+                    finish(l - 1, M, DEC, j)
 
                 @pl.when(i >= 1)
                 def _():
-                    qkv_block(l, part, chunks_of(i - 1))
+                    qkv_block(l, DEC, pair(i - 1))
             else:
-                qkv_block(l, part, chunks_of(i))
+                qkv_block(l, DEC, pair(i))
+
+                @pl.when(i == 2)
+                def _():
+                    for j in range(n_chunks):
+                        wo_copy(l, j).start()
             return c
 
         lax.fori_loop(0, steps, step, 0)
-        if arriving:
-            qkv_block(l, part, chunks_of(steps - 1))
+        if l > 0:
+            qkv_block(l, DEC, pair(steps - 1))
+        qkv_end(DEC)
+
+    def qkv_end(part):
+        r = whole(part)
         scale = next_scale(r)
         c_tab, s_tab = cos[r, :], sin[r, :]
 
@@ -225,7 +239,7 @@
             if part == DEC:
                 qs[pl.ds(h, dec, stride=heads), :] = q.astype(F32)
             else:
-                qp[:, h * hd:(h + 1) * hd] = q
+                att[dec:, h * hd:(h + 1) * hd] = q
         for g in range(kv_heads):
             k = rope(head(heads + g))
             v = head(heads + kv_heads + g)
@@ -248,11 +262,6 @@
             for t in range(ATT_SLOTS):
                 wait(kv_copies(l, ATT_SLOTS * i + t))
                 slots.append(lax.rem(ATT_SLOTS * i + t, KV_SLOTS))
-            if l == 0:
-                @pl.when(i == 2)
-                def _():
-                    for j in range(n_chunks):
-                        wo_copy(l, j).start()
             scores = []
             for n in range(step_rows):
                 b = i * step_rows + n
@@ -296,9 +305,11 @@
         wait(kv_pre_copies(l))
         old = jnp.where(lax.broadcasted_iota(jnp.int32, (1, seq), 1) < lens[dec], 0.0, -jnp.inf)
         causal = jnp.where(lax.broadcasted_iota(jnp.int32, (chunk, chunk), 1) <= lax.broadcasted_iota(jnp.int32, (chunk, chunk), 0), 0.0, -jnp.inf)
-        causal = jnp.concatenate([causal] * group, axis=0)
-        for g in range(kv_heads):
-            q = jnp.concatenate([qp[:, (g * group + i) * hd:(g * group + i + 1) * hd] for i in range(group)], axis=0)
+        causal = jnp.concatenate([causal] * STACK, axis=0)
+        for first in range(0, heads, STACK):
+            g = first // group
+            cut = [slice((first + i) * hd, (first + i + 1) * hd) for i in range(STACK)]
+            q = jnp.concatenate([att[dec:, c] for c in cut], axis=0)
             kv_col = slice(g * hd, (g + 1) * hd)
             s = lax.dot_general(q, kpre[g], (((1,), (1,)), ((), ())), preferred_element_type=F32) * scale_qk + old
             t = lax.dot_general(q, kp[:, kv_col], (((1,), (1,)), ((), ())), preferred_element_type=F32) * scale_qk + causal
@@ -308,8 +319,8 @@
             inv = 1.0 / (jnp.sum(es, axis=-1, keepdims=True) + jnp.sum(et, axis=-1, keepdims=True))
             o = jnp.dot((es * inv).astype(BF16), vpre[g], preferred_element_type=F32)
             o += jnp.dot((et * inv).astype(BF16), vp[:, kv_col], preferred_element_type=F32)
-            for i in range(group):
-                att[dec:, (g * group + i) * hd:(g * group + i + 1) * hd] = o[i * chunk:(i + 1) * chunk].astype(BF16)
+            for i in range(STACK):
+                att[dec:, cut[i]] = o[i * chunk:(i + 1) * chunk].astype(BF16)
 
     def o_part(l, part):
         r = whole(part)
@@ -347,27 +358,37 @@
             def _():
                 g_copy(l, nxt, (G_SLOTS + m) % 2).start()
 
+        def make_ahead(j):
+            abuf[j % 2] = operand(pl.ds(0, rows), j)
+
         def first_block(part):
             r = whole(part)
             a = operand(r, 0)
             for m in range(2):
                 if part == DEC:
                     g_copy(l, 0, m).wait()
+                elif m == 1:
+                    h_wait(O, DEC, 1)
+                    h_wait(O, PRE, 1)
+                    make_ahead(1)
                 for n in range(ff // CW):
                     acc[r, m * ff + n * CW:m * ff + (n + 1) * CW] = jnp.dot(a, gbuf[m, :, n * CW:(n + 1) * CW], preferred_element_type=F32)
                 if part == PRE:
                     g_copy(l, (G_SLOTS + m) // 2, (G_SLOTS + m) % 2).start()
 
-        def block(j):
-            h_wait(O, DEC, j)
-            h_wait(O, PRE, j)
-            a = operand(pl.ds(0, rows), j)
+        def block(j, more):
             for m in range(2):
                 g_copy(l, j, m).wait()
                 slot = lax.rem(2 * j + m, G_SLOTS)
+                if m == 1 and more:
+                    h_wait(O, DEC, j + 1)
+                    h_wait(O, PRE, j + 1)
+                    make_ahead(j + 1)
+                a = abuf[j % 2]
                 for n in range(ff // CW):
                     acc[:, m * ff + n * CW:m * ff + (n + 1) * CW] += jnp.dot(a, gbuf[slot, :, n * CW:(n + 1) * CW], preferred_element_type=F32)
-                release(j, m)
+                if more:
+                    release(j, m)
 
             @pl.when(j >= n_chunks - D_SLOTS)
             def _():
@@ -391,18 +412,16 @@
         first_block(PRE)
 
         def step(j, c):
-            @pl.when(j + 1 < n_chunks)
+            @pl.when(j + 1 >= AHEAD)
             def _():
-                @pl.when(j + 1 >= AHEAD)
-                def _():
-                    finish(l, O, DEC, j + 1)
-
-                finish(l, O, PRE, j + 1)
-
-            block(j)
-            return c
-
-        lax.fori_loop(1, n_chunks, step, 0)
+                finish(l, O, DEC, j + 1)
+
+            finish(l, O, PRE, j + 1)
+            block(j, True)
+            return c
+
+        lax.fori_loop(1, n_chunks - 1, step, 0)
+        block(n_chunks - 1, False)
         scale = next_scale(pl.ds(0, rows))
 
         def act_step(n, c):
@@ -488,22 +507,28 @@
     ssq[...] = jnp.zeros_like(ssq)
     pl.semaphore_wait(barrier, 2)
 
-    for l in range(layers):
-        qkv_part(l, DEC)
-        decode_attention(l)
-        o_part(l, DEC)
+    def finish_pre(l, first, stop):
         if l > 0:
             def pre_step(j, c):
                 finish(l - 1, M, PRE, j)
                 return c
 
-            lax.fori_loop(0, n_chunks, pre_step, 0)
-            for j in range(GROUP, AHEAD):
-                pair_sum(O, DEC, j)
-        qkv_part(l, PRE)
-        if l == 0:
-            for j in range(GROUP, AHEAD):
-                pair_sum(O, DEC, j)
+            lax.fori_loop(first, stop, pre_step, 0)
+
+    for l in range(layers):
+        qkv_decode(l)
+        decode_attention(l)
+        finish_pre(l, 0, 5)
+        o_part(l, DEC)
+        finish_pre(l, 5, 8)
+        qkv_begin(PRE)
+        qkv_block(l, PRE, tuple(range(5)))
+        for j in range(GROUP, AHEAD):
+            pair_sum(O, DEC, j)
+        finish_pre(l, 8, 10)
+        qkv_block(l, PRE, (5, 6, 7))
+        qkv_block(l, PRE, (8, 9))
+        qkv_end(PRE)
         for i in range(G_SLOTS):
             g_copy(l, i // 2, i % 2).start()
         prefill_attention(l)
@@ -581,6 +606,7 @@
         scratch_shapes=[
             buf((G_SLOTS, CW, ff), BF16),
             buf((D_SLOTS, ff, CW), BF16),
+            buf((2, rows, CW), BF16),
             buf((rows, 2 * ff), F32),
             buf((rows, ff), BF16),
             buf((n_chunks, rows, CW), BF16),
@@ -600,10 +626,6 @@
             buf((dec * heads, hd), F32),
             buf((dec * heads, hd), F32),
             buf((dec * heads, hd), F32),
-            buf((chunk, q_cols), BF16),
-            buf((chunk, k_cols), BF16),
-            buf((chunk, k_cols), BF16),
-            buf((rows, q_cols), BF16),
             sem((n_chunks,)),
             sem((n_chunks,)),
             sem((G_SLOTS,)),

time: 158 us -> 155 us (0.981)
  Pallas kernels: 155 us -> 152 us
    pallas_call x1, Pallas kernels: 155 us -> 152 us  [step_call(): pl.pallas_call(functools.partial(step_kernel, (dec, chunk)), out_shape=ja...]
where the time goes in v6:
time: 155 us
  Pallas kernels  152 us (98%)
  local copies, waits for them, and re-layouts  3.18 us (2%)
    pallas_call x1, Pallas kernels, step_call(): pl.pallas_call(functools.partial(step_kernel, (dec, chunk)), out_shape=ja...  152 us
    unnamed x1, local copies, waits for them, and re-layouts  3.18 us

profile of v6, /device:TPU:0, one launch (start us, length us, event | category | flops | bytes accessed | tf_op | source)
XLA Modules:
  0.0 155.2 jit_solution(6321678111156008546)
XLA Ops:
  0.0 152.0 %decoder_step.1 = bf16[224,5120]{1,0:T(8,128)(2,1)} custom-call(s32[97]{0:T(128)} %lens.1, bf16[224,5120]{1,0:T(8,128)(2,1)} %x_in.1, f32[1,128]{1,0:T(1,128)} %constant.2.clone.freq, bf16[2,5120]{1,0:T(2,128)(2,1)} %gain_a.1, bf16[2,5120]{1,0:T(2,128)(2,1)} %gain_m.1, bf16[2,5120,1024]{2,1,0:T(8,128)(2,1)} %wq.1, bf16[2,5120,256]{2,1,0:T(8,128)(2,1)} %wk.1, ...), custom_call_target="tpu_custom_call" | custom-call | tf_op jit(solution)/shard_map/decoder_step/pallas_call | solution.py:601
  152.0 3.2 %copy.16 = bf16[224,5120]{1,0:T(8,128)(2,1)} copy(bf16[224,5120]{1,0:T(8,128)(2,1)} %decoder_step.1) | data formatting | bytes 4587520

commit v7 on v6

--- a/solution.py
+++ b/solution.py
@@ -19,7 +19,7 @@
 KV_SLOTS = 5
 KV_ROWS = 8
 ATT_SLOTS = 2
-AHEAD = 7
+AHEAD_FIRST, AHEAD = 8, 6
 STACK = 4
 GROUP = 5
 O, M = 0, 1
@@ -73,6 +73,9 @@
     kp = act.at[pl.ds(0, chunk), pl.ds(q_cols, k_cols)]
     vp = act.at[pl.ds(0, chunk), pl.ds(q_cols + k_cols, k_cols)]
 
+    def order(l):
+        return (PRE, DEC, AHEAD_FIRST) if l == 0 else (DEC, PRE, AHEAD)
+
     xbs = (xb_o, xb_m)
     hs = (h_o, h_m)
 
@@ -182,7 +185,7 @@
             vals = h_m[j, r, :].astype(F32)
             add_squares(r, vals)
             a.append((vals * pre[r, :1] * gain_a[l:l + 1, cols(j)].astype(F32)).astype(BF16))
-            if part == DEC:
+            if part == order(l)[0]:
                 qkv_wait(j)
         for n in range(n_qkv // CW):
             total = acc[r, n * CW:(n + 1) * CW]
@@ -194,8 +197,9 @@
     def qkv_begin(part):
         acc[whole(part), :n_qkv] = jnp.zeros((size[part], n_qkv), F32)
 
-    def qkv_decode(l):
-        qkv_begin(DEC)
+    def qkv_lead(l):
+        part = order(l)[0]
+        qkv_begin(part)
         steps = n_chunks // 2
 
         def pair(i):
@@ -204,24 +208,29 @@
         def step(i, c):
             if l > 0:
                 for j in pair(i):
-                    finish(l - 1, M, DEC, j)
+                    finish(l - 1, M, part, j)
 
                 @pl.when(i >= 1)
                 def _():
-                    qkv_block(l, DEC, pair(i - 1))
+                    qkv_block(l, part, pair(i - 1))
             else:
-                qkv_block(l, DEC, pair(i))
-
-                @pl.when(i == 2)
+                qkv_block(l, part, pair(i))
+
+                @pl.when(i == 1)
                 def _():
                     for j in range(n_chunks):
                         wo_copy(l, j).start()
+
+                @pl.when(i == 3)
+                def _():
+                    for n in range(KV_SLOTS):
+                        start(kv_copies(l, n))
             return c
 
         lax.fori_loop(0, steps, step, 0)
         if l > 0:
-            qkv_block(l, DEC, pair(steps - 1))
-        qkv_end(DEC)
+            qkv_block(l, part, pair(steps - 1))
+        qkv_end(part)
 
     def qkv_end(part):
         r = whole(part)
@@ -328,7 +337,7 @@
         def step(i, c):
             these = tuple(GROUP * i + t for t in range(GROUP))
             for j in these:
-                if part == DEC:
+                if part == order(l)[0]:
                     wo_copy(l, j).wait()
                 sent(l, O, part, j)
             for j in these:
@@ -346,6 +355,8 @@
         lax.fori_loop(0, n_chunks // GROUP, step, 0)
 
     def gate_up(l):
+        lead, trail, ahead = order(l)
+
         def operand(r, j):
             vals = h_o[j, r, :].astype(F32)
             add_squares(r, vals)
@@ -365,7 +376,7 @@
             r = whole(part)
             a = operand(r, 0)
             for m in range(2):
-                if part == DEC:
+                if part == lead:
                     g_copy(l, 0, m).wait()
                 elif m == 1:
                     h_wait(O, DEC, 1)
@@ -373,7 +384,7 @@
                     make_ahead(1)
                 for n in range(ff // CW):
                     acc[r, m * ff + n * CW:m * ff + (n + 1) * CW] = jnp.dot(a, gbuf[m, :, n * CW:(n + 1) * CW], preferred_element_type=F32)
-                if part == PRE:
+                if part == trail:
                     g_copy(l, (G_SLOTS + m) // 2, (G_SLOTS + m) % 2).start()
 
         def block(j, more):
@@ -394,29 +405,29 @@
             def _():
                 d_copy(l, j - (n_chunks - D_SLOTS)).start()
 
-        def dec_step(j, c):
-            finish(l, O, DEC, j)
-            return c
-
-        lax.fori_loop(0, GROUP, dec_step, 0)
+        def lead_step(j, c):
+            finish(l, O, lead, j)
+            return c
+
+        lax.fori_loop(0, GROUP, lead_step, 0)
         for j in range(GROUP, n_chunks):
-            if j >= AHEAD:
-                pair_sum(O, DEC, j)
-            pair_sum(O, PRE, j)
-        lax.fori_loop(GROUP, AHEAD, dec_step, 0)
-        finish(l, O, PRE, 0)
-        h_wait(O, DEC, 0)
-        first_block(DEC)
-        finish(l, O, PRE, 1)
-        h_wait(O, PRE, 0)
-        first_block(PRE)
+            if j >= ahead:
+                pair_sum(O, lead, j)
+            pair_sum(O, trail, j)
+        lax.fori_loop(GROUP, ahead, lead_step, 0)
+        finish(l, O, trail, 0)
+        h_wait(O, lead, 0)
+        first_block(lead)
+        finish(l, O, trail, 1)
+        h_wait(O, trail, 0)
+        first_block(trail)
 
         def step(j, c):
-            @pl.when(j + 1 >= AHEAD)
+            @pl.when(j + 1 >= ahead)
             def _():
-                finish(l, O, DEC, j + 1)
-
-            finish(l, O, PRE, j + 1)
+                finish(l, O, lead, j + 1)
+
+            finish(l, O, trail, j + 1)
             block(j, True)
             return c
 
@@ -480,8 +491,6 @@
         pl.semaphore_signal(barrier, inc=1, device_id=peer, device_id_type=MESH)
     for j in range(n_chunks):
         start(qkv_copies(0, j))
-    for i in range(KV_SLOTS):
-        start(kv_copies(0, i))
     start(kv_pre_copies(0))
     ssq[...] = jnp.zeros_like(ssq)
 
@@ -516,23 +525,29 @@
             lax.fori_loop(first, stop, pre_step, 0)
 
     for l in range(layers):
-        qkv_decode(l)
-        decode_attention(l)
+        lead, trail, ahead = order(l)
+        attend = (decode_attention, prefill_attention)
+        qkv_lead(l)
+        attend[lead](l)
         finish_pre(l, 0, 5)
-        o_part(l, DEC)
+        o_part(l, lead)
         finish_pre(l, 5, 8)
-        qkv_begin(PRE)
-        qkv_block(l, PRE, tuple(range(5)))
-        for j in range(GROUP, AHEAD):
-            pair_sum(O, DEC, j)
+        qkv_begin(trail)
+        qkv_block(l, trail, tuple(range(5)))
+        for j in range(GROUP, ahead):
+            pair_sum(O, lead, j)
         finish_pre(l, 8, 10)
-        qkv_block(l, PRE, (5, 6, 7))
-        qkv_block(l, PRE, (8, 9))
-        qkv_end(PRE)
-        for i in range(G_SLOTS):
-            g_copy(l, i // 2, i % 2).start()
-        prefill_attention(l)
-        o_part(l, PRE)
+        qkv_block(l, trail, (5, 6, 7))
+        qkv_block(l, trail, (8, 9))
+        qkv_end(trail)
+        if trail == PRE:
+            for i in range(G_SLOTS):
+                g_copy(l, i // 2, i % 2).start()
+        attend[trail](l)
+        if trail == DEC:
+            for i in range(G_SLOTS):
+                g_copy(l, i // 2, i % 2).start()
+        o_part(l, trail)
         gate_up(l)
         down(l)
 

time: 155 us -> 150 us (0.968)
  Pallas kernels: 152 us -> 147 us
    pallas_call x1, Pallas kernels: 152 us -> 147 us  [step_call(): pl.pallas_call(functools.partial(step_kernel, (dec, chunk)), out_shape=ja...]
where the time goes in v7:
time: 150 us
  Pallas kernels  147 us (98%)
  local copies, waits for them, and re-layouts  3.18 us (2%)
    pallas_call x1, Pallas kernels, step_call(): pl.pallas_call(functools.partial(step_kernel, (dec, chunk)), out_shape=ja...  147 us
    unnamed x1, local copies, waits for them, and re-layouts  3.18 us

profile of v7, /device:TPU:0, one launch (start us, length us, event | category | flops | bytes accessed | tf_op | source)
XLA Modules:
  0.0 150.0 jit_solution(15034973984629488755)
XLA Ops:
  0.0 146.8 %decoder_step.1 = bf16[224,5120]{1,0:T(8,128)(2,1)} custom-call(s32[97]{0:T(128)} %lens.1, bf16[224,5120]{1,0:T(8,128)(2,1)} %x_in.1, f32[1,128]{1,0:T(1,128)} %constant.2.clone.freq, bf16[2,5120]{1,0:T(2,128)(2,1)} %gain_a.1, bf16[2,5120]{1,0:T(2,128)(2,1)} %gain_m.1, bf16[2,5120,1024]{2,1,0:T(8,128)(2,1)} %wq.1, bf16[2,5120,256]{2,1,0:T(8,128)(2,1)} %wk.1, ...), custom_call_target="tpu_custom_call" | custom-call | tf_op jit(solution)/shard_map/decoder_step/pallas_call | solution.py:616
  146.8 3.2 %copy.16 = bf16[224,5120]{1,0:T(8,128)(2,1)} copy(bf16[224,5120]{1,0:T(8,128)(2,1)} %decoder_step.1) | data formatting | bytes 4587520

commit v8 on v7

--- a/solution.py
+++ b/solution.py
@@ -498,7 +498,7 @@
         cos[pl.ds(b, 1), :] = jnp.full((1, hd), lens[b], jnp.int32).astype(F32)
         return c
 
-    lax.fori_loop(0, dec, place, 0)
+    lax.fori_loop(0, dec, place, 0, unroll=8)
     cos[pl.ds(dec, chunk), :] = (lax.broadcasted_iota(jnp.int32, (chunk, hd), 0) + lens[dec]).astype(F32)
     angles = cos[...] * freq[...]
     low = lax.broadcasted_iota(jnp.int32, (rows, hd), 1) < hd // 2
@@ -514,7 +514,6 @@
     lax.fori_loop(0, n_chunks, sq_step, 0)
     pre[...] = jnp.broadcast_to(jnp.maximum(inv_rms(pl.ds(0, rows)), 1e-30), pre.shape)
     ssq[...] = jnp.zeros_like(ssq)
-    pl.semaphore_wait(barrier, 2)
 
     def finish_pre(l, first, stop):
         if l > 0:
@@ -529,6 +528,8 @@
         attend = (decode_attention, prefill_attention)
         qkv_lead(l)
         attend[lead](l)
+        if l == 0:
+            pl.semaphore_wait(barrier, 2)
         finish_pre(l, 0, 5)
         o_part(l, lead)
         finish_pre(l, 5, 8)

time: 150 us -> 150 us (level)
  no operation moved by 1% of the time
where the time goes in v8:
time: 150 us
  Pallas kernels  147 us (98%)
  local copies, waits for them, and re-layouts  3.18 us (2%)
    pallas_call x1, Pallas kernels, step_call(): pl.pallas_call(functools.partial(step_kernel, (dec, chunk)), out_shape=ja...  147 us
    unnamed x1, local copies, waits for them, and re-layouts  3.18 us

profile of v8, /device:TPU:0, one launch (start us, length us, event | category | flops | bytes accessed | tf_op | source)
XLA Modules:
  0.0 150.0 jit_solution(13220586997110918846)
XLA Ops:
  0.0 146.8 %decoder_step.1 = bf16[224,5120]{1,0:T(8,128)(2,1)} custom-call(s32[97]{0:T(128)} %lens.1, bf16[224,5120]{1,0:T(8,128)(2,1)} %x_in.1, f32[1,128]{1,0:T(1,128)} %constant.2.clone.freq, bf16[2,5120]{1,0:T(2,128)(2,1)} %gain_a.1, bf16[2,5120]{1,0:T(2,128)(2,1)} %gain_m.1, bf16[2,5120,1024]{2,1,0:T(8,128)(2,1)} %wq.1, bf16[2,5120,256]{2,1,0:T(8,128)(2,1)} %wk.1, ...), custom_call_target="tpu_custom_call" | custom-call | tf_op jit(solution)/shard_map/decoder_step/pallas_call | solution.py:617
  146.8 3.2 %copy.16 = bf16[224,5120]{1,0:T(8,128)(2,1)} copy(bf16[224,5120]{1,0:T(8,128)(2,1)} %decoder_step.1) | data formatting | bytes 4587520
